TPU v7x, 128 devices: a whole 4x4x4 slice. The times are simulated.
128 devices in a mesh: gx: 4 (over x), gy: 4 (over y), gz: 8 (over z, core).
Axes of the slice: x: 4, y: 4, z: 4, core: 2. Of those that a mesh axis runs over, the one named last changes fastest.
Arguments:
- fields: bfloat16 [16384, 2048], P(('gx', 'gy', 'gz')), may hold values from -6 to 6
- coordinates: float32 [3, 2097152], P(None, ('gx', 'gy', 'gz')), may hold values from -1 to 1
- element_rank: int32 [2097152, 1], P(('gx', 'gy', 'gz')), may hold values from 0 to 127; in each aligned block of 16384 rows (0 to 16383, 16384 to 32767, ...) at most 160 rows name the same one
- element_slot: int32 [2097152], P(('gx', 'gy', 'gz')), may hold values from 0 to 127
Outputs:
- samples: float32 [4, 2097152], P(None, ('gx', 'gy', 'gz'))
Inputs may be any that keep to these rules, and one draw needn't show every extreme that they name: `element_rank`: among the probes of one device no rank is named by more than 160 probes, and in some devices' blocks one rank is named by exactly 160.
All inputs are finite; a program needn't handle non-finite values.
Results may differ from a plain program's by a relative error of at most 0.0024.
Values sent between devices are 32-bit elements; how exact they have to be, the bound alone decides.
A program may use at most 64 MiB of HBM per device.

v0:
```python
import math

import jax
import jax.numpy as jnp
import numpy as np
from jax import lax
from jax.sharding import PartitionSpec as P

gll_points = np.array(
    [
        -1.0,
        -0.8717401485096066,
        -0.5917001814331423,
        -0.2092992179024789,
        0.2092992179024789,
        0.5917001814331423,
        0.8717401485096066,
        1.0,
    ]
)
gll_scale = np.array(
    [1.0 / np.prod([gll_points[a] - gll_points[b] for b in range(8) if b != a]) for a in range(8)]
)


def lagrange(coord):
    offsets = coord[None, :] - jnp.asarray(gll_points, coord.dtype)[:, None]
    weights = []
    for node_a in range(8):
        factor = jnp.ones_like(coord) * gll_scale[node_a]
        for node_b in range(8):
            if node_b != node_a:
                factor = factor * offsets[node_b]
        weights.append(factor)
    return jnp.stack(weights, axis=0)


def interpolate(payload, fields):
    total_rows = payload.shape[1]
    local_count = fields.shape[0]
    block_rows = math.gcd(total_rows, 2048)
    block_count = total_rows // block_rows
    element_ids = jnp.arange(local_count, dtype=jnp.int32)

    def one_block(block):
        weight_r = lagrange(block[0])
        weight_s = lagrange(block[1])
        weight_t = lagrange(block[2]).astype(jnp.bfloat16)
        slots_block = block[3].astype(jnp.int32)
        picker = (slots_block[:, None] == element_ids[None, :]).astype(jnp.bfloat16)
        gathered = jnp.dot(picker, fields, preferred_element_type=jnp.float32).astype(jnp.bfloat16)
        gathered = gathered.reshape(block_rows, 256, 8)
        along_t = jnp.einsum("nak,kn->na", gathered, weight_t, preferred_element_type=jnp.float32)
        along_t = along_t.reshape(block_rows, 4, 8, 8)
        along_s = jnp.einsum("nfij,jn->nfi", along_t, weight_s)
        return jnp.einsum("nfi,in->fn", along_s, weight_r)

    blocks = payload.reshape(4, block_count, block_rows).transpose(1, 0, 2)
    result = lax.map(one_block, blocks)
    return result.transpose(1, 0, 2).reshape(4, total_rows)


def local(fields, coordinates, element_rank, element_slot):
    devices = lax.axis_size(("gx", "gy", "gz"))
    probes = element_slot.shape[0]
    capacity = 5 * probes // (4 * devices)
    target = element_rank[:, 0]
    group_rows = math.gcd(probes, 512)
    group_count = probes // group_rows
    onehot = (target[:, None] == jnp.arange(devices, dtype=jnp.int32)[None, :]).astype(jnp.bfloat16)
    onehot = onehot.reshape(group_count, group_rows, devices)
    lower = jnp.arange(group_rows)
    triangle = (lower[:, None] >= lower[None, :]).astype(jnp.bfloat16)
    within = jnp.einsum("ij,bjd->bid", triangle, onehot, preferred_element_type=jnp.float32)
    totals = within[:, -1, :]
    offsets = jnp.cumsum(totals, axis=0) - totals
    counted = (within + offsets[:, None, :]) * onehot.astype(jnp.float32)
    position = (jnp.sum(counted, axis=2).reshape(probes) - 1.0).astype(jnp.int32)
    flat = target * capacity + position
    payload = jnp.concatenate([coordinates, element_slot.astype(jnp.float32)[None, :]], axis=0)
    send = jnp.zeros((4, devices * capacity), jnp.float32).at[:, flat].set(payload)
    arrived = lax.all_to_all(
        send.reshape(4, devices, capacity),
        ("gx", "gy", "gz"),
        split_axis=1,
        concat_axis=1,
        tiled=True,
    )
    width = arrived.shape[2]
    values = interpolate(arrived.reshape(4, -1), fields)
    values = values.reshape(4, devices, width)
    returned = lax.all_to_all(values, ("gx", "gy", "gz"), split_axis=1, concat_axis=1, tiled=True)
    return returned.reshape(4, devices * capacity)[:, flat]


def solution(mesh):
    placed = (
        P(("gx", "gy", "gz"), None),
        P(None, ("gx", "gy", "gz")),
        P(("gx", "gy", "gz"), None),
        P(("gx", "gy", "gz")),
    )
    return jax.shard_map(
        local, mesh=mesh, in_specs=placed, out_specs=P(None, ("gx", "gy", "gz")), check_vma=False
    )
```

profile of v0, /device:TPU:1, one launch (start us, length us, event | category | flops | bytes accessed | tf_op | source)
XLA Modules:
  0.0 285.1 jit_solution(4110278924828847493)
XLA Ops:
  0.0 0.5 broadcast.166
  0.5 1.6 reduce.11
  2.2 2.4 fusion.9
  4.6 3.2 %copy-done = f32[32,512,128]{1,2,0:T(8,128)} copy-done((f32[32,512,128]{1,2,0:T(8,128)}, f32[32,512,128]{1,2,0:T(8,128)S(1)}, u32[]{:S(2)}) %copy-start) | copy-done | bytes 8388632
  7.8 0.6 slice.374
  8.4 0.6 copy.30
  9.1 0.6 copy.31
  9.7 2.8 subtract_reduce_fusion
  12.5 4.5 %multiply_reduce_fusion.3 = f32[32,512]{1,0:T(8,128)S(1)} fusion(f32[32,512,128]{1,2,0:T(8,128)} %copy-done, f32[32,128]{1,0:T(8,128)S(1)} %subtract_reduce_fusion, s32[32,512]{1,0:T(8,128)S(1)} %eq.30), kind=kLoop, calls=%fused_computation.42 | loop fusion | flops 12566528 | bytes 8536064 | tf_op jit(solution)/shard_map/reduce_sum | solution.py:78
  17.3 0.1 maximum_bitcast_fusion
  17.4 5.1 %copy.32 = f32[16384,4]{1,0:T(8,128)} copy(f32[16384,4]{0,1:T(4,128)S(1)} %maximum_bitcast_fusion) | data formatting | bytes 524288 | tf_op jit(solution)/shard_map/concatenate | solution.py:80
  22.5 45.3 %scatter_custom_fusion = f32[4,20480]{0,1:T(8,128)} fusion(s32[16384]{0:T(1024)S(1)} %bitcast.88, f32[16384,4]{1,0:T(8,128)} %copy.32, f32[]{:T(128)} %constant.13.clone.1), kind=kCustom, calls=%fused_computation.46 | custom fusion | bytes 328192 | tf_op jit(solution)/shard_map/scatter | solution.py:81
  67.9 8.0 %copy.33 = f32[4,128,160]{2,0,1:T(4,128)} copy(f32[4,128,160]{0,2,1:T(8,128)} %bitcast.78) | data formatting | bytes 655360 | tf_op jit(solution)/shard_map/reshape | solution.py:83
  75.8 11.5 %all-to-all-start = ((f32[4,128,160]{2,0,1:T(4,128)}), f32[4,128,160]{2,0,1:T(4,128)S(1)}, u32[]{:S(2)}, u32[]{:S(2)}) async-start(f32[4,128,160]{2,0,1:T(4,128)} %copy.33), calls=%async_computation | async-start | bytes 1048576 | tf_op jit(solution)/shard_map/all_to_all | solution.py:82
  87.3 13.5 %all-to-all-done = f32[4,128,160]{2,0,1:T(4,128)S(1)} async-done(((f32[4,128,160]{2,0,1:T(4,128)}), f32[4,128,160]{2,0,1:T(4,128)S(1)}, u32[]{:S(2)}, u32[]{:S(2)}) %all-to-all-start) | async-done | bytes 327712 | tf_op jit(solution)/shard_map/all_to_all | solution.py:82
  101.0 0.4 reshape_reshape.6
  101.4 93.6 %while.13 = (s32[]{:T(128)}, f32[10,4,2048]{2,1,0:T(4,128)S(1)}, f32[10,4,2048]{2,0,1:T(8,128)S(1)}, bf16[128,2048]{1,0:T(8,128)(2,1)}, s32[]{:T(128)}, /*index=5*/f32[8]{0:T(128)S(1)}, s32[]{:T(128)}, s32[]{}, s32[]{}, s32[]{}) while((s32[]{:T(128)}, f32[10,4,2048]{2,1,0:T(4,128)S(1)}, ...), condition=%wide.region_4.5_spmd.clone.clone.clone, body=%wide.region_3.4_spmd.sunk.clone.clone.clone.sunk | while | flops 1091790848 | bytes 7209149 | solution.py:59
  102.0 7.2 %multiply_reduce_fusion.7 = f32[2048,256]{0,1:T(8,128)S(1)} fusion(f32[2048,8]{0,1:T(8,128)S(1)} %bitcast_convert_fusion.2, bf16[128,2048]{1,0:T(8,128)(2,1)} %get-tuple-element.256, s32[2048]{0:T(1024)S(1)} %bitcast.92), kind=kOutput, calls=%fused_computation.3.clone.1 | convolution fusion | flops 1090256896 | bytes 2695168 | tf_op jit(solution)/shard_map/while/body/eval_jaxpr/dot_general | solution.py:51
  109.4 0.1 stack.22
  109.5 0.7 multiply_reduce_fusion.8
  110.5 0.1 stack.24
  111.3 7.2 %multiply_reduce_fusion.7 = f32[2048,256]{0,1:T(8,128)S(1)} fusion(f32[2048,8]{0,1:T(8,128)S(1)} %bitcast_convert_fusion.2, bf16[128,2048]{1,0:T(8,128)(2,1)} %get-tuple-element.256, s32[2048]{0:T(1024)S(1)} %bitcast.92), kind=kOutput, calls=%fused_computation.3.clone.1 | convolution fusion | flops 1090256896 | bytes 2695168 | tf_op jit(solution)/shard_map/while/body/eval_jaxpr/dot_general | solution.py:51
  118.8 0.1 stack.22
  118.9 0.7 multiply_reduce_fusion.8
  119.9 0.1 stack.24
  120.7 7.2 %multiply_reduce_fusion.7 = f32[2048,256]{0,1:T(8,128)S(1)} fusion(f32[2048,8]{0,1:T(8,128)S(1)} %bitcast_convert_fusion.2, bf16[128,2048]{1,0:T(8,128)(2,1)} %get-tuple-element.256, s32[2048]{0:T(1024)S(1)} %bitcast.92), kind=kOutput, calls=%fused_computation.3.clone.1 | convolution fusion | flops 1090256896 | bytes 2695168 | tf_op jit(solution)/shard_map/while/body/eval_jaxpr/dot_general | solution.py:51
  128.2 0.1 stack.22
  128.3 0.7 multiply_reduce_fusion.8
  129.3 0.1 stack.24
  130.1 7.2 %multiply_reduce_fusion.7 = f32[2048,256]{0,1:T(8,128)S(1)} fusion(f32[2048,8]{0,1:T(8,128)S(1)} %bitcast_convert_fusion.2, bf16[128,2048]{1,0:T(8,128)(2,1)} %get-tuple-element.256, s32[2048]{0:T(1024)S(1)} %bitcast.92), kind=kOutput, calls=%fused_computation.3.clone.1 | convolution fusion | flops 1090256896 | bytes 2695168 | tf_op jit(solution)/shard_map/while/body/eval_jaxpr/dot_general | solution.py:51
  137.5 0.1 stack.22
  137.6 0.7 multiply_reduce_fusion.8
  138.6 0.1 stack.24
  139.4 7.2 %multiply_reduce_fusion.7 = f32[2048,256]{0,1:T(8,128)S(1)} fusion(f32[2048,8]{0,1:T(8,128)S(1)} %bitcast_convert_fusion.2, bf16[128,2048]{1,0:T(8,128)(2,1)} %get-tuple-element.256, s32[2048]{0:T(1024)S(1)} %bitcast.92), kind=kOutput, calls=%fused_computation.3.clone.1 | convolution fusion | flops 1090256896 | bytes 2695168 | tf_op jit(solution)/shard_map/while/body/eval_jaxpr/dot_general | solution.py:51
  146.9 0.1 stack.22
  147.0 0.7 multiply_reduce_fusion.8
  148.0 0.1 stack.24
  148.8 7.2 %multiply_reduce_fusion.7 = f32[2048,256]{0,1:T(8,128)S(1)} fusion(f32[2048,8]{0,1:T(8,128)S(1)} %bitcast_convert_fusion.2, bf16[128,2048]{1,0:T(8,128)(2,1)} %get-tuple-element.256, s32[2048]{0:T(1024)S(1)} %bitcast.92), kind=kOutput, calls=%fused_computation.3.clone.1 | convolution fusion | flops 1090256896 | bytes 2695168 | tf_op jit(solution)/shard_map/while/body/eval_jaxpr/dot_general | solution.py:51
  156.3 0.1 stack.22
  156.4 0.7 multiply_reduce_fusion.8
  157.4 0.1 stack.24
  158.2 7.2 %multiply_reduce_fusion.7 = f32[2048,256]{0,1:T(8,128)S(1)} fusion(f32[2048,8]{0,1:T(8,128)S(1)} %bitcast_convert_fusion.2, bf16[128,2048]{1,0:T(8,128)(2,1)} %get-tuple-element.256, s32[2048]{0:T(1024)S(1)} %bitcast.92), kind=kOutput, calls=%fused_computation.3.clone.1 | convolution fusion | flops 1090256896 | bytes 2695168 | tf_op jit(solution)/shard_map/while/body/eval_jaxpr/dot_general | solution.py:51
  165.6 0.1 stack.22
  165.7 0.7 multiply_reduce_fusion.8
  166.7 0.1 stack.24
  167.5 7.2 %multiply_reduce_fusion.7 = f32[2048,256]{0,1:T(8,128)S(1)} fusion(f32[2048,8]{0,1:T(8,128)S(1)} %bitcast_convert_fusion.2, bf16[128,2048]{1,0:T(8,128)(2,1)} %get-tuple-element.256, s32[2048]{0:T(1024)S(1)} %bitcast.92), kind=kOutput, calls=%fused_computation.3.clone.1 | convolution fusion | flops 1090256896 | bytes 2695168 | tf_op jit(solution)/shard_map/while/body/eval_jaxpr/dot_general | solution.py:51
  175.0 0.1 stack.22
  175.1 0.7 multiply_reduce_fusion.8
  176.1 0.1 stack.24
  176.9 7.2 %multiply_reduce_fusion.7 = f32[2048,256]{0,1:T(8,128)S(1)} fusion(f32[2048,8]{0,1:T(8,128)S(1)} %bitcast_convert_fusion.2, bf16[128,2048]{1,0:T(8,128)(2,1)} %get-tuple-element.256, s32[2048]{0:T(1024)S(1)} %bitcast.92), kind=kOutput, calls=%fused_computation.3.clone.1 | convolution fusion | flops 1090256896 | bytes 2695168 | tf_op jit(solution)/shard_map/while/body/eval_jaxpr/dot_general | solution.py:51
  184.3 0.1 stack.22
  184.5 0.7 multiply_reduce_fusion.8
  185.5 0.1 stack.24
  186.3 7.2 %multiply_reduce_fusion.7 = f32[2048,256]{0,1:T(8,128)S(1)} fusion(f32[2048,8]{0,1:T(8,128)S(1)} %bitcast_convert_fusion.2, bf16[128,2048]{1,0:T(8,128)(2,1)} %get-tuple-element.256, s32[2048]{0:T(1024)S(1)} %bitcast.92), kind=kOutput, calls=%fused_computation.3.clone.1 | convolution fusion | flops 1090256896 | bytes 2695168 | tf_op jit(solution)/shard_map/while/body/eval_jaxpr/dot_general | solution.py:51
  193.7 0.1 stack.22
  193.8 0.7 multiply_reduce_fusion.8
  195.0 0.2 copy.36
  195.3 0.3 reshape_reshape.7
  195.6 1.1 copy.37
  196.7 4.7 %all-to-all-start.1 = ((f32[4,128,160]{2,0,1:T(4,128)}), f32[4,128,160]{2,0,1:T(4,128)S(1)}, u32[]{:S(2)}, u32[]{:S(2)}) async-start(f32[4,128,160]{2,0,1:T(4,128)} %copy.37), calls=%async_computation.1 | async-start | bytes 1048576 | tf_op jit(solution)/shard_map/all_to_all | solution.py:92
  201.4 13.6 %all-to-all-done.1 = f32[4,128,160]{2,0,1:T(4,128)S(1)} async-done(((f32[4,128,160]{2,0,1:T(4,128)}), f32[4,128,160]{2,0,1:T(4,128)S(1)}, u32[]{:S(2)}, u32[]{:S(2)}) %all-to-all-start.1) | async-done | bytes 327712 | tf_op jit(solution)/shard_map/all_to_all | solution.py:92
  215.0 5.7 %copy.38 = f32[4,128,160]{0,2,1:T(8,128)} copy(f32[4,128,160]{2,0,1:T(4,128)S(1)} %all-to-all-done.1) | data formatting | bytes 655360 | tf_op jit(solution)/shard_map/all_to_all | solution.py:92
  220.7 58.5 %gather_fusion = f32[16384,4]{1,0:T(8,128)} fusion(f32[4,20480]{0,1:T(8,128)} %bitcast.79, s32[16384]{0:T(1024)S(1)} %broadcast_clamp_fusion), kind=kCustom, calls=%fused_computation | custom fusion | bytes 589824 | tf_op jit(solution)/shard_map/gather | solution.py:93
  279.2 5.9 %copy.39 = f32[4,16384]{1,0:T(4,128)} copy(f32[4,16384]{0,1:T(8,128)} %bitcast.80) | data formatting | bytes 524288 | tf_op jit(solution)/shard_map/gather | solution.py:93
  (199 shorter events, 12.1 us)
Async XLA Ops:
  4.6 3.2 %copy-start = (f32[32,512,128]{1,2,0:T(8,128)}, f32[32,512,128]{1,2,0:T(8,128)S(1)}, u32[]{:S(2)}) copy-start(f32[32,512,128]{1,2,0:T(8,128)S(1)} %fusion.9) | copy-start | bytes 25165828
  8.4 8.8 %copy-start.1 = (s32[16384,1]{0,1:T(1,128)S(1)}, s32[16384,1]{0,1:T(1,128)}, u32[]{:S(2)}) copy-start(s32[16384,1]{0,1:T(1,128)} %param.11) | copy-start | bytes 196612
  8.4 8.9 %copy-start.3 = (s32[16384]{0:T(1024)S(1)}, s32[16384]{0:T(1024)}, u32[]{:S(2)}) copy-start(s32[16384]{0:T(1024)} %param.12) | copy-start | bytes 196612
  8.4 8.9 %copy-start.2 = (f32[3,16384]{1,0:T(4,128)S(1)}, f32[3,16384]{1,0:T(4,128)}, u32[]{:S(2)}) copy-start(f32[3,16384]{1,0:T(4,128)} %param.10) | copy-start | bytes 589828
  67.9 33.5 %copy-start.4 = (f32[8]{0:T(128)S(1)}, f32[8]{0:T(128)}, u32[]{:S(2)}) copy-start(f32[8]{0:T(128)} %constant.81) | copy-start | bytes 100
  75.8 25.0 %all-to-all-start = ((f32[4,128,160]{2,0,1:T(4,128)}), f32[4,128,160]{2,0,1:T(4,128)S(1)}, u32[]{:S(2)}, u32[]{:S(2)}) async-start(f32[4,128,160]{2,0,1:T(4,128)} %copy.33), calls=%async_computation | async-start | bytes 1048576 | tf_op jit(solution)/shard_map/all_to_all | solution.py:82
  196.7 18.3 %all-to-all-start.1 = ((f32[4,128,160]{2,0,1:T(4,128)}), f32[4,128,160]{2,0,1:T(4,128)S(1)}, u32[]{:S(2)}, u32[]{:S(2)}) async-start(f32[4,128,160]{2,0,1:T(4,128)} %copy.37), calls=%async_computation.1 | async-start | bytes 1048576 | tf_op jit(solution)/shard_map/all_to_all | solution.py:92
where the time goes:
time: 286 us; the launch traced here: 285 us
  local copies, waits for them, and re-layouts  140 us (49%)
  matrix products  73.9 us (26%)
  waiting for transfers between devices  27.1 us (9%)
  other arithmetic  26.5 us (9%)
  starting transfers between devices  16.2 us (6%)
    dot_general x10, matrix products, one_block(): jnp.dot(picker, fields, preferred_element_type=jnp.float32)  71.5 us
    gather x2, local copies, waits for them, and re-layouts, local(): return returned.reshape(4, devices * capacity)[:, flat]  64.4 us
    scatter x1, local copies, waits for them, and re-layouts, local(): jnp.zeros((4, devices * capacity), jnp.float32).at[:, flat].set(payload)  45.3 us
    all_to_all x1, waiting for transfers between devices, local(): lax.all_to_all(values, ('gx', 'gy', 'gz'), split_axis=1, concat_axis=1, t...  13.6 us
    all_to_all x1, waiting for transfers between devices, local(): lax.all_to_all(send.reshape(4, devices, capacity), ('gx', 'gy', 'gz'), sp...  13.5 us
    all_to_all x1, starting transfers between devices, local(): lax.all_to_all(send.reshape(4, devices, capacity), ('gx', 'gy', 'gz'), sp...  11.5 us
    reshape x1, local copies, waits for them, and re-layouts, local(): send.reshape(4, devices, capacity)  7.96 us
    dot_general x10, other arithmetic, one_block(): along_s = jnp.einsum('nfij,jn->nfi', along_t, weight_s)  6.96 us
  transfers between devices with their start and end apart: 2, of which 2 were waited for; matrix products, arithmetic and copies ran while one was open for 0% of the time, Pallas kernels for 0%

commit v1 on v0

v1 whole, which is shorter than its diff:
```python
import jax
import jax.numpy as jnp
import numpy as np
from jax import lax
from jax.experimental import pallas as pl
from jax.experimental.pallas import tpu as pltpu
from jax.sharding import PartitionSpec as P

AXES = ("gx", "gy", "gz")
NV = 16

gll_points = np.array(
    [
        -1.0,
        -0.8717401485096066,
        -0.5917001814331423,
        -0.2092992179024789,
        0.2092992179024789,
        0.5917001814331423,
        0.8717401485096066,
        1.0,
    ]
)
gll_scale = np.array(
    [1.0 / np.prod([gll_points[a] - gll_points[b] for b in range(8) if b != a]) for a in range(8)]
)


def iotas():
    return lax.broadcasted_iota(jnp.int32, (8, 128), 0), lax.broadcasted_iota(jnp.int32, (8, 128), 1)


def partner(x, axis, d, bit):
    n = x.shape[axis]
    if 2 * d == n:
        return pltpu.roll(x, d, axis)
    if axis == 1:
        idx = lax.broadcasted_iota(jnp.int32, x.shape, 1) ^ d
        return jnp.take_along_axis(x, idx, axis=1)
    return jnp.where(bit, pltpu.roll(x, d, axis), pltpu.roll(x, n - d, axis))


def network(arrs):
    s_io, l_io = iotas()
    arrs = [list(a) for a in arrs]
    count = len(arrs)

    def bit_of(b):
        if b < 7:
            return ((s_io >> (b - 4)) & 1) == 1
        return ((l_io >> (b - 7)) & 1) == 1

    for k in range(1, 15):
        down = bit_of(k) if 4 <= k < 14 else None
        for j in range(k - 1, 3, -1):
            axis, d = (0, 1 << (j - 4)) if j < 7 else (1, 1 << (j - 7))
            upper = bit_of(j)
            flip = upper if down is None else jnp.logical_xor(upper, down)
            for v in range(NV):
                other = [partner(arrs[a][v], axis, d, upper) for a in range(count)]
                take = jnp.logical_xor(arrs[0][v] > other[0], flip)
                for a in range(count):
                    arrs[a][v] = jnp.where(take, other[a], arrs[a][v])
        for j in range(min(k, 4) - 1, -1, -1):
            d = 1 << j
            for v in range(NV):
                if v & d:
                    continue
                w = v | d
                if k < 4 and (v >> k) & 1:
                    swap = arrs[0][v] < arrs[0][w]
                else:
                    swap = arrs[0][v] > arrs[0][w]
                if down is not None:
                    swap = jnp.logical_xor(swap, down)
                for a in range(count):
                    x, y = arrs[a][v], arrs[a][w]
                    arrs[a][v] = jnp.where(swap, y, x)
                    arrs[a][w] = jnp.where(swap, x, y)
    return arrs


def take_lanes(x, idx):
    return jnp.take_along_axis(x, idx, axis=1)


def rows_up(low, high, d, s_io):
    return jnp.where(s_io < 8 - d, pltpu.roll(low, 8 - d, 0), pltpu.roll(high, 8 - d, 0))


def rows_down(low, high, d, s_io):
    return jnp.where(s_io >= d, pltpu.roll(high, d, 0), pltpu.roll(low, d, 0))


def dispatch_kernel(rank_ref, slot_ref, coord_ref, send_ref, key_ref, meta_ref):
    s_io, l_io = iotas()
    keys = []
    for v in range(NV):
        label = l_io * 128 + s_io * 16 + v
        keys.append(rank_ref[v] * (1 << 21) + slot_ref[v] * (1 << 14) + label)
    coords = [[coord_ref[c, v] for v in range(NV)] for c in range(3)]
    keys, *coords = network([keys] + coords)
    for v in range(NV):
        key_ref[v] = keys[v]
    last = (keys[NV - 1][7:8, :] >> 21).astype(jnp.float32)
    last = jnp.broadcast_to(last, (128, 128)).T
    lanes = lax.broadcasted_iota(jnp.int32, (128, 128), 1).astype(jnp.float32)
    column = jnp.sum((last < lanes).astype(jnp.float32), axis=0, keepdims=True)
    column = jnp.broadcast_to(column, (8, 128)).astype(jnp.int32)
    columns = [jnp.minimum(column + k, 127) for k in range(3)]
    spread = [[take_lanes(keys[v], columns[k]) for v in range(NV)] for k in range(3)]
    below = jnp.zeros((8, 128), jnp.float32)
    for v in range(NV):
        below = below + ((spread[0][v] >> 21) < l_io).astype(jnp.float32)
    shift = jnp.broadcast_to(jnp.sum(below, axis=0, keepdims=True), (8, 128)).astype(jnp.int32)
    meta_ref[0] = column
    meta_ref[1] = shift

    tails = []
    for a in range(4):
        if a == 3:
            table = [[((x >> 14) & 127).astype(jnp.float32) for x in block] for block in spread]
        else:
            table = [[take_lanes(coords[a][v], columns[k]) for v in range(NV)] for k in range(3)]
        for b in range(4):
            d = 1 << b
            bit = ((shift >> b) & 1) == 1
            moved = []
            for k in range(3):
                row = []
                for v in range(NV):
                    if v + d < NV:
                        src = table[k][v + d]
                    else:
                        src = rows_up(table[k][v + d - NV], table[min(k + 1, 2)][v + d - NV], 1, s_io)
                    row.append(jnp.where(bit, src, table[k][v]))
                moved.append(row)
            table = moved
        for b in range(4, 7):
            d = 1 << (b - 4)
            bit = ((shift >> b) & 1) == 1
            moved = [
                [
                    jnp.where(bit, rows_up(table[k][v], table[min(k + 1, len(table) - 1)][v], d, s_io), table[k][v])
                    for v in range(NV)
                ]
                for k in range(2)
            ]
            table = moved
        send_ref[a] = jnp.concatenate(table[0], axis=0).T
        for q in range(4):
            tail = table[1][4 * q]
            for u in range(1, 4):
                tail = jnp.where(s_io >= 2 * u, pltpu.roll(table[1][4 * q + u], 2 * u, 0), tail)
            tails.append(tail)
    send_ref[4] = jnp.concatenate(tails, axis=0).T


def return_kernel(back_ref, key_ref, meta_ref, out_ref):
    s_io, l_io = iotas()
    column, shift = meta_ref[0], meta_ref[1]
    keys = [key_ref[v] for v in range(NV)]
    ranks = [x >> 21 for x in keys]
    blocks = [l_io - take_lanes(column, x) for x in ranks]
    tails = back_ref[4].T
    values = []
    for f in range(4):
        main = back_ref[f].T
        first = [main[8 * v : 8 * v + 8] for v in range(NV)]
        second = []
        for v in range(NV):
            q, u = v // 4, v % 4
            at = f * 32 + q * 8
            x = tails[at : at + 8]
            second.append(pltpu.roll(x, 8 - 2 * u, 0) if u else x)
        table = [first, second, second]
        for b in range(6, 3, -1):
            d = 1 << (b - 4)
            bit = ((shift >> b) & 1) == 1
            table = [
                [jnp.where(bit, rows_down(table[max(k - 1, 0)][v], table[k][v], d, s_io), table[k][v]) for v in range(NV)]
                for k in range(3)
            ]
        for b in range(3, -1, -1):
            d = 1 << b
            bit = ((shift >> b) & 1) == 1
            moved = []
            for k in range(3):
                row = []
                for v in range(NV):
                    if v >= d:
                        src = table[k][v - d]
                    else:
                        src = rows_down(table[max(k - 1, 0)][v - d + NV], table[k][v - d + NV], 1, s_io)
                    row.append(jnp.where(bit, src, table[k][v]))
                moved.append(row)
            table = moved
        picked = []
        for v in range(NV):
            x = [take_lanes(table[k][v], ranks[v]) for k in range(3)]
            picked.append(jnp.where(blocks[v] == 0, x[0], jnp.where(blocks[v] == 1, x[1], x[2])))
        values.append(picked)
    labels = [x & 16383 for x in keys]
    _, *values = network([labels] + values)
    for f in range(4):
        for v in range(NV):
            out_ref[f, v] = values[f][v]


def node_weights(coord):
    node = lax.broadcasted_iota(jnp.int32, (8, coord.shape[1]), 0)
    scale = jnp.full(node.shape, float(gll_scale[0]), jnp.float32)
    for a in range(1, 8):
        scale = jnp.where(node == a, float(gll_scale[a]), scale)
    factors = [jnp.where(node == b, 1.0, coord - float(gll_points[b])) for b in range(8)]
    while len(factors) > 1:
        factors = [factors[i] * factors[i + 1] for i in range(0, len(factors), 2)]
    return factors[0] * scale


def interpolate_kernel(got_ref, fields_ref, out_ref, tail_ref):
    sources = got_ref.shape[1]
    lane = lax.broadcasted_iota(jnp.int32, (sources // 4, 128), 1) >> 5
    ends = [got_ref[4, pl.ds(w, sources // 4, stride=4), :] for w in range(4)]
    tails = []
    for a in range(4):
        row = None
        for w in range(4):
            turn = (32 * (w - a)) % 128
            x = pltpu.roll(ends[w], turn, 1) if turn else ends[w]
            row = x if row is None else jnp.where(lane == w, x, row)
        tails.append(row)
    rows = sources + sources // 4
    element = lax.broadcasted_iota(jnp.int32, (128, 256), 0)

    def row_of(a, i):
        if i < sources:
            return got_ref[a, i : i + 1, :]
        return tails[a][i - sources : i - sources + 1, :]

    results = []
    for i in range(0, rows, 2):
        r, s, t, slot = [jnp.concatenate([row_of(a, i), row_of(a, i + 1)], axis=1) for a in range(4)]
        weight_r, weight_s, weight_t = node_weights(r), node_weights(s), node_weights(t)
        onehot = (element == slot.astype(jnp.int32)).astype(jnp.float32).astype(jnp.bfloat16)
        onehot = onehot.reshape(8, 16, 256)
        parts = []
        for c in range(8):
            w = jnp.broadcast_to(weight_t[c : c + 1], (16, 256)).astype(jnp.bfloat16)
            parts.append((onehot * w[None]).reshape(128, 256))
        picker = jnp.concatenate(parts, axis=0)
        along = jnp.dot(fields_ref[...], picker, preferred_element_type=jnp.float32)
        along = along.reshape(4, 8, 8, 256)
        along = jnp.sum(along * weight_r[None, :, None, :], axis=1)
        value = jnp.sum(along * weight_s[None], axis=1)
        for h in range(2):
            for f in range(4):
                piece = value[f : f + 1, 128 * h : 128 * h + 128]
                if i + h < sources:
                    out_ref[f, i + h : i + h + 1, :] = piece
                else:
                    tail_ref[f, i + h - sources : i + h - sources + 1, :] = piece
    for w in range(4):
        row = None
        for f in range(4):
            turn = (32 * (f - w)) % 128
            x = tail_ref[f, 0 : sources // 4, :]
            x = pltpu.roll(x, turn, 1) if turn else x
            row = x if row is None else jnp.where(lane == f, x, row)
        out_ref[4, pl.ds(w, sources // 4, stride=4), :] = row


def dispatch(rank, slot, coords):
    return pl.pallas_call(
        dispatch_kernel,
        out_shape=[
            jax.ShapeDtypeStruct((5, 128, 128), jnp.float32),
            jax.ShapeDtypeStruct((NV, 8, 128), jnp.int32),
            jax.ShapeDtypeStruct((2, 8, 128), jnp.int32),
        ],
        name="dispatch",
    )(rank, slot, coords)


def interpolate(got, table, chunk=32):
    return pl.pallas_call(
        interpolate_kernel,
        grid=(128 // chunk,),
        in_specs=[
            pl.BlockSpec((5, chunk, 128), lambda i: (0, i, 0)),
            pl.BlockSpec((256, 1024), lambda i: (0, 0)),
        ],
        out_specs=pl.BlockSpec((5, chunk, 128), lambda i: (0, i, 0)),
        out_shape=jax.ShapeDtypeStruct((5, 128, 128), jnp.float32),
        scratch_shapes=[pltpu.VMEM((4, 8, 128), jnp.float32)],
        name="interpolate",
    )(got, table)


def give_back(back, key, meta):
    return pl.pallas_call(
        return_kernel,
        out_shape=jax.ShapeDtypeStruct((4, NV, 8, 128), jnp.float32),
        name="give_back",
    )(back, key, meta)


def local(fields, coordinates, element_rank, element_slot):
    rank = element_rank.reshape(NV, 8, 128)
    slot = element_slot.reshape(NV, 8, 128)
    coords = coordinates.reshape(3, NV, 8, 128)
    table = fields.reshape(128, 256, 8).transpose(1, 2, 0).reshape(256, 1024)
    send, key, meta = dispatch(rank, slot, coords)
    got = lax.all_to_all(send, AXES, split_axis=1, concat_axis=1, tiled=True)
    values = interpolate(got, table)
    back = lax.all_to_all(values, AXES, split_axis=1, concat_axis=1, tiled=True)
    return give_back(back, key, meta).reshape(4, 16384)


def solution(mesh):
    placed = (P(AXES, None), P(None, AXES), P(AXES, None), P(AXES))
    return jax.shard_map(local, mesh=mesh, in_specs=placed, out_specs=P(None, AXES), check_vma=False)
```

time: 286 us -> 78.1 us (0.27)
  local copies, waits for them, and re-layouts: 140 us -> 9.33 us
  matrix products: 73.9 us -> 0 us
  other arithmetic: 26.5 us -> 0 us
  Pallas kernels: 0 us -> 26.4 us
  blocking collectives: 0 us -> 18.1 us
  waiting for transfers between devices: 27.1 us -> 12.4 us
  starting transfers between devices: 16.2 us -> 11.5 us
    dot_general x11 -> x0, matrix products: 73.9 us -> none  [the longest x10 71.5 us: one_block(): jnp.dot(picker, fields, preferred_element_type=jnp.float32)]
    gather x2 -> x0, local copies, waits for them, and re-layouts: 64.4 us -> none  [local(): return returned.reshape(4, devices * capacity)[:, flat]]
    scatter x1 -> x0, local copies, waits for them, and re-layouts: 45.3 us -> none  [local(): jnp.zeros((4, devices * capacity), jnp.float32).at[:, flat].set(payload)]
    pallas_call x0 -> x3, Pallas kernels: none -> 26.4 us  [the longest x1 14.1 us: interpolate(): pl.pallas_call(interpolate_kernel, grid=(128 // chunk,), in_specs=[pl.Blo...]
    all_to_all x0 -> x1, blocking collectives: none -> 18.1 us  [local(): back = lax.all_to_all(values, AXES, split_axis=1, concat_axis=1, tiled=True)]
    all_to_all x2 -> x1, waiting for transfers between devices: 27.1 us -> 12.4 us  [local(): got = lax.all_to_all(send, AXES, split_axis=1, concat_axis=1, tiled=True)]
    reshape x1 -> x0, local copies, waits for them, and re-layouts: 7.96 us -> none  [local(): send.reshape(4, devices, capacity)]
    dot_general x20 -> x0, other arithmetic: 7.86 us -> none  [the longest x10 6.96 us: one_block(): along_s = jnp.einsum('nfij,jn->nfi', along_t, weight_s)]
  transfers between devices with their start and end apart: 2 -> 1, of which waited for: 2 -> 1; matrix products, arithmetic and copies ran while one was open for 0% -> 1% of each run, Pallas kernels for 0% -> 0%
where the time goes in v1:
time: 78.1 us; the launch traced here: 77.7 us
  Pallas kernels  26.4 us (34%)
  blocking collectives  18.1 us (23%)
  waiting for transfers between devices  12.4 us (16%)
  starting transfers between devices  11.5 us (15%)
  local copies, waits for them, and re-layouts  9.33 us (12%)
    all_to_all x1, blocking collectives, local(): back = lax.all_to_all(values, AXES, split_axis=1, concat_axis=1, tiled=True)  18.1 us
    pallas_call x1, Pallas kernels, interpolate(): pl.pallas_call(interpolate_kernel, grid=(128 // chunk,), in_specs=[pl.Blo...  14.1 us
    all_to_all x1, waiting for transfers between devices, local(): got = lax.all_to_all(send, AXES, split_axis=1, concat_axis=1, tiled=True)  12.4 us
    all_to_all x1, starting transfers between devices, local(): got = lax.all_to_all(send, AXES, split_axis=1, concat_axis=1, tiled=True)  11.5 us
    pallas_call x1, Pallas kernels, give_back(): pl.pallas_call(return_kernel, out_shape=jax.ShapeDtypeStruct((4, NV, 8, 1...  6.52 us
    pallas_call x1, Pallas kernels, dispatch(): pl.pallas_call(dispatch_kernel, out_shape=[jax.ShapeDtypeStruct((5, 128,...  5.86 us
    unnamed x6, local copies, waits for them, and re-layouts  4.63 us
    pallas_call x1, local copies, waits for them, and re-layouts, dispatch(): pl.pallas_call(dispatch_kernel, out_shape=[jax.ShapeDtypeStruct((5, 128,...  1.96 us
  transfers between devices with their start and end apart: 1, of which 1 were waited for; matrix products, arithmetic and copies ran while one was open for 1% of the time, Pallas kernels for 0%

profile of v1, /device:TPU:1, one launch (start us, length us, event | category | flops | bytes accessed | tf_op | source)
XLA Modules:
  0.0 77.7 jit_solution(14785410954776428049)
XLA Ops:
  0.0 1.6 %copy.20 = f32[1,3,128,128]{3,2,1,0:T(8,128)} copy(f32[1,3,128,128]{3,1,2,0:T(4,128)} %bitcast.23) | data formatting | bytes 393216
  1.6 5.9 %dispatch.1 = (f32[5,128,128]{2,1,0:T(8,128)}, s32[16,8,128]{2,1,0:T(8,128)}, s32[2,8,128]{2,1,0:T(8,128)}) custom-call(s32[16,8,128]{2,1,0:T(8,128)} %bitcast.24, s32[16,8,128]{2,1,0:T(8,128)} %bitcast.25, f32[3,16,8,128]{3,2,1,0:T(8,128)} %bitcast.22), custom_call_target="tpu_custom_call" | custom-call | tf_op jit(solution)/shard_map/dispatch/pallas_call | solution.py:274
  7.5 2.0 %copy.7 = f32[5,128,128]{2,0,1:T(8,128)} copy(f32[5,128,128]{2,1,0:T(8,128)} %get-tuple-element.8) | data formatting | bytes 655360 | tf_op jit(solution)/shard_map/dispatch/pallas_call | solution.py:274
  9.5 0.0 copy-start
  9.5 11.5 %all-to-all-start = ((f32[5,128,128]{2,0,1:T(8,128)}), f32[5,128,128]{2,0,1:T(8,128)S(1)}, u32[]{:S(2)}, u32[]{:S(2)}) async-start(f32[5,128,128]{2,0,1:T(8,128)} %copy.7), calls=%async_computation | async-start | bytes 1048576 | tf_op jit(solution)/shard_map/all_to_all | solution.py:314
  21.0 0.0 copy-done
  21.0 0.3 copy.8
  21.2 0.9 %copy.18 = bf16[32,8,8,128]{3,1,2,0:T(8,128)(2,1)} copy(bf16[32,8,8,128]{3,2,1,0:T(8,128)(2,1)S(1)} %bitcast.20) | data formatting | bytes 1048576
  22.1 12.4 %all-to-all-done = f32[5,128,128]{2,0,1:T(8,128)S(1)} async-done(((f32[5,128,128]{2,0,1:T(8,128)}), f32[5,128,128]{2,0,1:T(8,128)S(1)}, u32[]{:S(2)}, u32[]{:S(2)}) %all-to-all-start) | async-done | bytes 327712 | tf_op jit(solution)/shard_map/all_to_all | solution.py:314
  34.5 0.8 %copy.9.got_ref = f32[5,128,128]{2,1,0:T(8,128)} copy(f32[5,128,128]{2,0,1:T(8,128)S(1)} %all-to-all-done) | data formatting | bytes 655360 | tf_op jit(solution)/shard_map/all_to_all | solution.py:314
  35.3 14.1 %interpolate.1 = f32[5,128,128]{2,1,0:T(8,128)} custom-call(f32[5,128,128]{2,1,0:T(8,128)} %copy.9.got_ref, bf16[256,1024]{1,0:T(8,128)(2,1)} %bitcast.19), custom_call_target="tpu_custom_call" | custom-call | tf_op jit(solution)/shard_map/interpolate/pallas_call | solution.py:286
  49.4 1.2 %copy.10 = f32[5,128,128]{2,0,1:T(8,128)S(1)} copy(f32[5,128,128]{2,1,0:T(8,128)} %interpolate.1) | data formatting | bytes 655360 | tf_op jit(solution)/shard_map/interpolate/pallas_call | solution.py:286
  50.5 18.1 %all_to_all.10 = f32[5,128,128]{2,0,1:T(8,128)S(1)} all-to-all(f32[5,128,128]{2,0,1:T(8,128)S(1)} %copy.10), channel_id=1, replica_groups=mesh['gx'=4,'gy'=4,'gz'=8] {'gx','gy','gz'}, dimensions={1} | all-to-all | bytes 655360 | tf_op jit(solution)/shard_map/all_to_all | solution.py:316
  68.6 0.8 %copy.11.back_ref = f32[5,128,128]{2,1,0:T(8,128)} copy(f32[5,128,128]{2,0,1:T(8,128)S(1)} %all_to_all.10) | data formatting | bytes 655360 | tf_op jit(solution)/shard_map/all_to_all | solution.py:316
  69.4 6.5 %give_back.1 = f32[4,16,8,128]{3,2,1,0:T(8,128)} custom-call(f32[5,128,128]{2,1,0:T(8,128)} %copy.11.back_ref, s32[16,8,128]{2,1,0:T(8,128)} %get-tuple-element.9.key_ref, s32[2,8,128]{2,1,0:T(8,128)} %get-tuple-element.10.meta_ref), custom_call_target="tpu_custom_call" | custom-call | tf_op jit(solution)/shard_map/give_back/pallas_call | solution.py:301
  75.9 1.8 %copy.19 = f32[1,4,128,128]{3,1,2,0:T(4,128)} copy(f32[1,4,128,128]{3,2,1,0:T(8,128)} %bitcast.21) | data formatting | bytes 524288
Async XLA Ops:
  9.5 11.5 %copy-start = (bf16[128,2048]{1,0:T(8,128)(2,1)S(1)}, bf16[128,2048]{1,0:T(8,128)(2,1)}, u32[]{:S(2)}) copy-start(bf16[128,2048]{1,0:T(8,128)(2,1)} %param.4) | copy-start | bytes 1572868
  9.5 25.0 %all-to-all-start = ((f32[5,128,128]{2,0,1:T(8,128)}), f32[5,128,128]{2,0,1:T(8,128)S(1)}, u32[]{:S(2)}, u32[]{:S(2)}) async-start(f32[5,128,128]{2,0,1:T(8,128)} %copy.7), calls=%async_computation | async-start | bytes 1048576 | tf_op jit(solution)/shard_map/all_to_all | solution.py:314

commit v2 on v1

--- a/solution.py
+++ b/solution.py
@@ -7,6 +7,8 @@
 from jax.sharding import PartitionSpec as P
 
 AXES = ("gx", "gy", "gz")
+MESH = pl.DeviceIdType.MESH
+CHUNK = 16
 NV = 16
 
 gll_points = np.array(
@@ -218,56 +220,129 @@
     return factors[0] * scale
 
 
-def interpolate_kernel(got_ref, fields_ref, out_ref, tail_ref):
-    sources = got_ref.shape[1]
-    lane = lax.broadcasted_iota(jnp.int32, (sources // 4, 128), 1) >> 5
-    ends = [got_ref[4, pl.ds(w, sources // 4, stride=4), :] for w in range(4)]
-    tails = []
-    for a in range(4):
-        row = None
-        for w in range(4):
-            turn = (32 * (w - a)) % 128
-            x = pltpu.roll(ends[w], turn, 1) if turn else ends[w]
-            row = x if row is None else jnp.where(lane == w, x, row)
-        tails.append(row)
-    rows = sources + sources // 4
+def offsets(slot):
+    return (slot // 4) % 4, slot % 4, slot // 16
+
+
+def exchange_kernel(send, table, back, got, vals, send_sem, got_sems, value_sem, back_sem):
+    gx, gy, gz = (lax.axis_index(name) for name in AXES)
+    me = gx * 32 + gy * 8 + gz
+
+    def ahead(slot):
+        dx, dy, dz = offsets(slot)
+        return (gx + dx) % 4, (gy + dy) % 4, (gz + dz) % 8
+
+    def behind(slot):
+        dx, dy, dz = offsets(slot)
+        return (gx + 4 - dx) % 4, (gy + 4 - dy) % 4, (gz + 8 - dz) % 8
+
+    def number(where):
+        return where[0] * 32 + where[1] * 8 + where[2]
+
+    barrier = pltpu.get_barrier_semaphore()
+
+    def greet(slot, carry):
+        pl.semaphore_signal(barrier, inc=1, device_id=ahead(slot), device_id_type=MESH)
+        return carry
+
+    lax.fori_loop(1, 128, greet, 0)
+    pl.semaphore_wait(barrier, 127)
+
+    pltpu.make_async_copy(send.at[:, me], got.at[:, 0], got_sems.at[0]).start()
+
+    def ship(slot, carry):
+        where = ahead(slot)
+        pltpu.make_async_remote_copy(
+            src_ref=send.at[:, number(where)],
+            dst_ref=got.at[:, slot],
+            send_sem=send_sem,
+            recv_sem=got_sems.at[slot // CHUNK],
+            device_id=where,
+            device_id_type=MESH,
+        ).start()
+        return carry
+
+    lax.fori_loop(1, 128, ship, 0)
+
+    lane = lax.broadcasted_iota(jnp.int32, (1, 128), 1) >> 5
     element = lax.broadcasted_iota(jnp.int32, (128, 256), 0)
 
-    def row_of(a, i):
-        if i < sources:
-            return got_ref[a, i : i + 1, :]
-        return tails[a][i - sources : i - sources + 1, :]
-
-    results = []
-    for i in range(0, rows, 2):
-        r, s, t, slot = [jnp.concatenate([row_of(a, i), row_of(a, i + 1)], axis=1) for a in range(4)]
-        weight_r, weight_s, weight_t = node_weights(r), node_weights(s), node_weights(t)
-        onehot = (element == slot.astype(jnp.int32)).astype(jnp.float32).astype(jnp.bfloat16)
-        onehot = onehot.reshape(8, 16, 256)
-        parts = []
-        for c in range(8):
-            w = jnp.broadcast_to(weight_t[c : c + 1], (16, 256)).astype(jnp.bfloat16)
-            parts.append((onehot * w[None]).reshape(128, 256))
-        picker = jnp.concatenate(parts, axis=0)
-        along = jnp.dot(fields_ref[...], picker, preferred_element_type=jnp.float32)
-        along = along.reshape(4, 8, 8, 256)
-        along = jnp.sum(along * weight_r[None, :, None, :], axis=1)
-        value = jnp.sum(along * weight_s[None], axis=1)
-        for h in range(2):
-            for f in range(4):
-                piece = value[f : f + 1, 128 * h : 128 * h + 128]
-                if i + h < sources:
-                    out_ref[f, i + h : i + h + 1, :] = piece
+    def work(chunk, carry):
+        base = chunk * CHUNK
+        block = got.at[:, pl.ds(base, CHUNK)]
+        pltpu.make_async_copy(block, block, got_sems.at[chunk]).wait()
+        rows = [[got[a, base + i] for a in range(4)] for i in range(CHUNK)]
+        for i in range(CHUNK // 4):
+            ends = [got[4, base + 4 * i + w] for w in range(4)]
+            tail = []
+            for a in range(4):
+                row = None
+                for w in range(4):
+                    turn = (32 * (w - a)) % 128
+                    x = pltpu.roll(ends[w], turn, 1) if turn else ends[w]
+                    row = x if row is None else jnp.where(lane == w, x, row)
+                tail.append(row)
+            rows.append(tail)
+        found = []
+        for i in range(0, len(rows), 2):
+            r, s, t, slot = [jnp.concatenate([rows[i][a], rows[i + 1][a]], axis=1) for a in range(4)]
+            weight_r, weight_s, weight_t = node_weights(r), node_weights(s), node_weights(t)
+            onehot = (element == slot.astype(jnp.int32)).astype(jnp.float32).astype(jnp.bfloat16)
+            onehot = onehot.reshape(8, 16, 256)
+            parts = []
+            for c in range(8):
+                w = jnp.broadcast_to(weight_t[c : c + 1], (16, 256)).astype(jnp.bfloat16)
+                parts.append((onehot * w[None]).reshape(128, 256))
+            picker = jnp.concatenate(parts, axis=0)
+            along = jnp.dot(table[...], picker, preferred_element_type=jnp.float32)
+            along = along.reshape(4, 8, 8, 256)
+            along = jnp.sum(along * weight_r[None, :, None, :], axis=1)
+            value = jnp.sum(along * weight_s[None], axis=1)
+            for h in range(2):
+                pieces = [value[f : f + 1, 128 * h : 128 * h + 128] for f in range(4)]
+                if i + h < CHUNK:
+                    for f in range(4):
+                        vals[f, base + i + h] = pieces[f]
                 else:
-                    tail_ref[f, i + h - sources : i + h - sources + 1, :] = piece
-    for w in range(4):
-        row = None
-        for f in range(4):
-            turn = (32 * (f - w)) % 128
-            x = tail_ref[f, 0 : sources // 4, :]
-            x = pltpu.roll(x, turn, 1) if turn else x
-            row = x if row is None else jnp.where(lane == f, x, row)
-        out_ref[4, pl.ds(w, sources // 4, stride=4), :] = row
+                    found.append(pieces)
+        for i in range(CHUNK // 4):
+            for w in range(4):
+                row = None
+                for f in range(4):
+                    turn = (32 * (f - w)) % 128
+                    x = pltpu.roll(found[i][f], turn, 1) if turn else found[i][f]
+                    row = x if row is None else jnp.where(lane == f, x, row)
+                vals[4, base + 4 * i + w] = row
+
+        def answer(slot, inner):
+            where = behind(slot)
+
+            @pl.when(slot == 0)
+            def _():
+                pltpu.make_async_copy(vals.at[:, 0], back.at[:, me], back_sem).start()
+
+            @pl.when(slot > 0)
+            def _():
+                pltpu.make_async_remote_copy(
+                    src_ref=vals.at[:, slot],
+                    dst_ref=back.at[:, me],
+                    send_sem=value_sem,
+                    recv_sem=back_sem,
+                    device_id=where,
+                    device_id_type=MESH,
+                ).start()
+
+            return inner
+
+        lax.fori_loop(base, base + CHUNK, answer, 0)
+        return carry
+
+    lax.fori_loop(0, 128 // CHUNK, work, 0)
+    sent = send.at[:, pl.ds(0, 127)]
+    pltpu.make_async_copy(sent, sent, send_sem).wait()
+    told = vals.at[:, pl.ds(0, 127)]
+    pltpu.make_async_copy(told, told, value_sem).wait()
+    pltpu.make_async_copy(back, back, back_sem).wait()
 
 
 def dispatch(rank, slot, coords):
@@ -282,19 +357,23 @@
     )(rank, slot, coords)
 
 
-def interpolate(got, table, chunk=32):
+def exchange(send, table):
     return pl.pallas_call(
-        interpolate_kernel,
-        grid=(128 // chunk,),
-        in_specs=[
-            pl.BlockSpec((5, chunk, 128), lambda i: (0, i, 0)),
-            pl.BlockSpec((256, 1024), lambda i: (0, 0)),
+        exchange_kernel,
+        in_specs=[pl.BlockSpec(memory_space=pltpu.VMEM)] * 2,
+        out_specs=pl.BlockSpec(memory_space=pltpu.VMEM),
+        out_shape=jax.ShapeDtypeStruct((5, 128, 1, 128), jnp.float32),
+        scratch_shapes=[
+            pltpu.VMEM((5, 128, 1, 128), jnp.float32),
+            pltpu.VMEM((5, 128, 1, 128), jnp.float32),
+            pltpu.SemaphoreType.DMA,
+            pltpu.SemaphoreType.DMA((128 // CHUNK,)),
+            pltpu.SemaphoreType.DMA,
+            pltpu.SemaphoreType.DMA,
         ],
-        out_specs=pl.BlockSpec((5, chunk, 128), lambda i: (0, i, 0)),
-        out_shape=jax.ShapeDtypeStruct((5, 128, 128), jnp.float32),
-        scratch_shapes=[pltpu.VMEM((4, 8, 128), jnp.float32)],
-        name="interpolate",
-    )(got, table)
+        compiler_params=pltpu.CompilerParams(collective_id=0, has_side_effects=True),
+        name="exchange",
+    )(send, table)
 
 
 def give_back(back, key, meta):
@@ -311,9 +390,7 @@
     coords = coordinates.reshape(3, NV, 8, 128)
     table = fields.reshape(128, 256, 8).transpose(1, 2, 0).reshape(256, 1024)
     send, key, meta = dispatch(rank, slot, coords)
-    got = lax.all_to_all(send, AXES, split_axis=1, concat_axis=1, tiled=True)
-    values = interpolate(got, table)
-    back = lax.all_to_all(values, AXES, split_axis=1, concat_axis=1, tiled=True)
+    back = exchange(send.reshape(5, 128, 1, 128), table).reshape(5, 128, 128)
     return give_back(back, key, meta).reshape(4, 16384)
 
 

time: 78.1 us -> 57.8 us (0.74)
  Pallas kernels: 26.4 us -> 52.9 us
  blocking collectives: 18.1 us -> 0 us
  waiting for transfers between devices: 12.4 us -> 0 us
  starting transfers between devices: 11.5 us -> 0 us
  local copies, waits for them, and re-layouts: 9.33 us -> 4.68 us
    pallas_call x1, Pallas kernels: 14.1 us -> 40.5 us  [exchange(): pl.pallas_call(exchange_kernel, in_specs=[pl.BlockSpec(memory_space=pltpu...]
    all_to_all x1 -> x0, blocking collectives: 18.1 us -> none  [local(): back = lax.all_to_all(values, AXES, split_axis=1, concat_axis=1, tiled=True)]
    all_to_all x1 -> x0, waiting for transfers between devices: 12.4 us -> none  [local(): got = lax.all_to_all(send, AXES, split_axis=1, concat_axis=1, tiled=True)]
    all_to_all x1 -> x0, starting transfers between devices: 11.5 us -> none  [local(): got = lax.all_to_all(send, AXES, split_axis=1, concat_axis=1, tiled=True)]
    pallas_call x2 -> x0, local copies, waits for them, and re-layouts: 3.14 us -> none  [the longest x1 1.96 us: dispatch(): pl.pallas_call(dispatch_kernel, out_shape=[jax.ShapeDtypeStruct((5, 128,...]
    all_to_all x2 -> x0, local copies, waits for them, and re-layouts: 1.57 us -> none  [the longest x1 0.79 us: local(): got = lax.all_to_all(send, AXES, split_axis=1, concat_axis=1, tiled=True)]
  transfers between devices with their start and end apart: 1 -> 0, of which waited for: 1 -> 0; matrix products, arithmetic and copies ran while one was open for 1% -> 0% of each run, Pallas kernels for 0% -> 0%
where the time goes in v2:
time: 57.8 us; the launch traced here: 57.6 us
  Pallas kernels  52.9 us (92%)
  local copies, waits for them, and re-layouts  4.68 us (8%)
    pallas_call x1, Pallas kernels, exchange(): pl.pallas_call(exchange_kernel, in_specs=[pl.BlockSpec(memory_space=pltpu...  40.5 us
    pallas_call x1, Pallas kernels, give_back(): pl.pallas_call(return_kernel, out_shape=jax.ShapeDtypeStruct((4, NV, 8, 1...  6.51 us
    pallas_call x1, Pallas kernels, dispatch(): pl.pallas_call(dispatch_kernel, out_shape=[jax.ShapeDtypeStruct((5, 128,...  5.85 us
    unnamed x6, local copies, waits for them, and re-layouts  4.68 us

profile of v2, /device:TPU:1, one launch (start us, length us, event | category | flops | bytes accessed | tf_op | source)
XLA Modules:
  0.0 57.6 jit_solution(9409561850046235652)
XLA Ops:
  0.0 0.0 copy-start
  0.0 1.7 %copy.15 = f32[1,3,128,128]{3,2,1,0:T(8,128)} copy(f32[1,3,128,128]{3,1,2,0:T(4,128)} %bitcast.27) | data formatting | bytes 393216
  1.7 5.9 %dispatch.1 = (f32[5,128,128]{2,1,0:T(8,128)}, s32[16,8,128]{2,1,0:T(8,128)}, s32[2,8,128]{2,1,0:T(8,128)}) custom-call(s32[16,8,128]{2,1,0:T(8,128)} %bitcast.28, s32[16,8,128]{2,1,0:T(8,128)} %bitcast.29, f32[3,16,8,128]{3,2,1,0:T(8,128)} %bitcast.25), custom_call_target="tpu_custom_call" | custom-call | tf_op jit(solution)/shard_map/dispatch/pallas_call | solution.py:349
  7.6 0.0 copy-done
  7.6 0.3 copy.6
  7.8 0.9 %copy.13 = bf16[32,8,8,128]{3,1,2,0:T(8,128)(2,1)} copy(bf16[32,8,8,128]{3,2,1,0:T(8,128)(2,1)S(1)} %bitcast.22) | data formatting | bytes 1048576
  8.7 40.5 %exchange.1 = f32[5,128,1,128]{3,2,1,0:T(1,128)} custom-call(f32[5,128,1,128]{3,2,1,0:T(1,128)} %bitcast.26, bf16[256,1024]{1,0:T(8,128)(2,1)} %bitcast.21), custom_call_target="tpu_custom_call" | custom-call | tf_op jit(solution)/shard_map/exchange/pallas_call | solution.py:361
  49.2 6.5 %give_back.1 = f32[4,16,8,128]{3,2,1,0:T(8,128)} custom-call(f32[5,128,128]{2,1,0:T(8,128)} %bitcast.23, s32[16,8,128]{2,1,0:T(8,128)} %get-tuple-element.9.key_ref, s32[2,8,128]{2,1,0:T(8,128)} %get-tuple-element.10.meta_ref), custom_call_target="tpu_custom_call" | custom-call | tf_op jit(solution)/shard_map/give_back/pallas_call | solution.py:380
  55.7 1.8 %copy.14 = f32[1,4,128,128]{3,1,2,0:T(4,128)} copy(f32[1,4,128,128]{3,2,1,0:T(8,128)} %bitcast.24) | data formatting | bytes 524288
Async XLA Ops:
  0.0 7.6 %copy-start = (bf16[128,2048]{1,0:T(8,128)(2,1)S(1)}, bf16[128,2048]{1,0:T(8,128)(2,1)}, u32[]{:S(2)}) copy-start(bf16[128,2048]{1,0:T(8,128)(2,1)} %param.4) | copy-start | bytes 1572868

commit v3 on v2

--- a/solution.py
+++ b/solution.py
@@ -1,3 +1,5 @@
+import functools
+
 import jax
 import jax.numpy as jnp
 import numpy as np
@@ -7,8 +9,9 @@
 from jax.sharding import PartitionSpec as P
 
 AXES = ("gx", "gy", "gz")
-MESH = pl.DeviceIdType.MESH
+LOGICAL = pl.DeviceIdType.LOGICAL
 CHUNK = 16
+LEVELS = (1 << 21) - 1
 NV = 16
 
 gll_points = np.array(
@@ -94,14 +97,29 @@
     return jnp.where(s_io >= d, pltpu.roll(high, d, 0), pltpu.roll(low, d, 0))
 
 
-def dispatch_kernel(rank_ref, slot_ref, coord_ref, send_ref, key_ref, meta_ref):
+def hold(x):
+    return ((x + 1.0) * (LEVELS / 2) + 0.5).astype(jnp.int32)
+
+
+def release(q):
+    return q.astype(jnp.float32) * (2 / LEVELS) - 1.0
+
+
+def right(x, count):
+    return lax.shift_right_logical(x, jnp.full(x.shape, count, jnp.int32))
+
+
+def dispatch_steps(rank_ref, slot_ref, coord_ref, send_ref, key_ref, meta_ref):
     s_io, l_io = iotas()
-    keys = []
+    words = [[], [], []]
     for v in range(NV):
         label = l_io * 128 + s_io * 16 + v
-        keys.append(rank_ref[v] * (1 << 21) + slot_ref[v] * (1 << 14) + label)
-    coords = [[coord_ref[c, v] for v in range(NV)] for c in range(3)]
-    keys, *coords = network([keys] + coords)
+        r, s, t = [hold(coord_ref[8 * v : 8 * v + 8, c, :]) for c in range(3)]
+        words[0].append(rank_ref[v] * (1 << 21) + slot_ref[v] * (1 << 14) + label)
+        words[1].append((r << 11) | (t >> 10))
+        words[2].append((s << 11) | (t & 1023))
+    words = network(words)
+    keys = words[0]
     for v in range(NV):
         key_ref[v] = keys[v]
     last = (keys[NV - 1][7:8, :] >> 21).astype(jnp.float32)
@@ -118,12 +136,9 @@
     meta_ref[0] = column
     meta_ref[1] = shift
 
-    tails = []
-    for a in range(4):
-        if a == 3:
-            table = [[((x >> 14) & 127).astype(jnp.float32) for x in block] for block in spread]
-        else:
-            table = [[take_lanes(coords[a][v], columns[k]) for v in range(NV)] for k in range(3)]
+    moved_words = []
+    for a in range(3):
+        table = spread if a == 0 else [[take_lanes(words[a][v], columns[k]) for v in range(NV)] for k in range(3)]
         for b in range(4):
             d = 1 << b
             bit = ((shift >> b) & 1) == 1
@@ -141,21 +156,30 @@
         for b in range(4, 7):
             d = 1 << (b - 4)
             bit = ((shift >> b) & 1) == 1
-            moved = [
+            table = [
                 [
                     jnp.where(bit, rows_up(table[k][v], table[min(k + 1, len(table) - 1)][v], d, s_io), table[k][v])
                     for v in range(NV)
                 ]
                 for k in range(2)
             ]
-            table = moved
-        send_ref[a] = jnp.concatenate(table[0], axis=0).T
+        rows = list(table[0])
         for q in range(4):
             tail = table[1][4 * q]
             for u in range(1, 4):
                 tail = jnp.where(s_io >= 2 * u, pltpu.roll(table[1][4 * q + u], 2 * u, 0), tail)
-            tails.append(tail)
-    send_ref[4] = jnp.concatenate(tails, axis=0).T
+            rows.append(tail)
+        moved_words.append(rows)
+    key, first, second = moved_words
+    split = [
+        [release(right(x, 11)) for x in first],
+        [release(right(x, 11)) for x in second],
+        [release(((x & 2047) << 10) | (y & 1023)) for x, y in zip(first, second)],
+        [((x >> 14) & 127).astype(jnp.float32) for x in key],
+    ]
+    for a in range(4):
+        send_ref[a] = jnp.concatenate(split[a][:NV], axis=0).T
+    send_ref[4] = jnp.concatenate([x for a in range(4) for x in split[a][NV:]], axis=0).T
 
 
 def return_kernel(back_ref, key_ref, meta_ref, out_ref):
@@ -202,11 +226,28 @@
             x = [take_lanes(table[k][v], ranks[v]) for k in range(3)]
             picked.append(jnp.where(blocks[v] == 0, x[0], jnp.where(blocks[v] == 1, x[1], x[2])))
         values.append(picked)
-    labels = [x & 16383 for x in keys]
-    _, *values = network([labels] + values)
-    for f in range(4):
-        for v in range(NV):
-            out_ref[f, v] = values[f][v]
+    largest = functools.reduce(jnp.maximum, [jnp.abs(x) for picked in values for x in picked])
+    largest = jnp.maximum(jnp.max(jnp.max(largest, axis=0, keepdims=True), axis=1, keepdims=True), 1e-30)
+    grow = jnp.broadcast_to(524287.0 / largest, (8, 128))
+    shrink = jnp.broadcast_to(largest / 524287.0, (8, 128))
+    words = [[], [], []]
+    for v in range(NV):
+        q = [(values[f][v] * grow + 524288.5).astype(jnp.int32) for f in range(4)]
+        low = ((q[0] & 15) << 12) | ((q[1] & 15) << 8) | ((q[2] & 15) << 4) | (q[3] & 15)
+        words[0].append(((keys[v] & 16383) << 16) | low)
+        words[1].append(((q[0] >> 4) << 16) | (q[1] >> 4))
+        words[2].append(((q[2] >> 4) << 16) | (q[3] >> 4))
+    words = network(words)
+    for v in range(NV):
+        low, first, second = [words[a][v] for a in range(3)]
+        q = [
+            (right(first, 16) << 4) | ((low >> 12) & 15),
+            ((first & 65535) << 4) | ((low >> 8) & 15),
+            (right(second, 16) << 4) | ((low >> 4) & 15),
+            ((second & 65535) << 4) | (low & 15),
+        ]
+        for f in range(4):
+            out_ref[8 * v : 8 * v + 8, f, :] = (q[f] - 524288).astype(jnp.float32) * shrink
 
 
 def node_weights(coord):
@@ -220,49 +261,40 @@
     return factors[0] * scale
 
 
-def offsets(slot):
-    return (slot // 4) % 4, slot % 4, slot // 16
-
-
-def exchange_kernel(send, table, back, got, vals, send_sem, got_sems, value_sem, back_sem):
+def exchange_kernel(
+    rank_ref, slot_ref, coord_ref, table, back, key_ref, meta_ref, send, got, vals, send_sem, got_sems, value_sem, back_sem
+):
     gx, gy, gz = (lax.axis_index(name) for name in AXES)
     me = gx * 32 + gy * 8 + gz
 
-    def ahead(slot):
-        dx, dy, dz = offsets(slot)
-        return (gx + dx) % 4, (gy + dy) % 4, (gz + dz) % 8
-
-    def behind(slot):
-        dx, dy, dz = offsets(slot)
-        return (gx + 4 - dx) % 4, (gy + 4 - dy) % 4, (gz + 8 - dz) % 8
-
-    def number(where):
-        return where[0] * 32 + where[1] * 8 + where[2]
-
+    def ahead(dx, dy, dz):
+        return ((gx + dx) % 4) * 32 + ((gy + dy) % 4) * 8 + (gz + dz) % 8
+
+    def behind(dx, dy, dz):
+        return ((gx + 4 - dx) % 4) * 32 + ((gy + 4 - dy) % 4) * 8 + (gz + 8 - dz) % 8
+
+    def steps(chunk, half):
+        dx = chunk // 2
+        return dx, ((chunk + dx) % 2) * 2 + half
+
+    targets = [ahead(*steps(slot // 16, (slot // 8) % 2), slot % 8) for slot in range(128)]
     barrier = pltpu.get_barrier_semaphore()
-
-    def greet(slot, carry):
-        pl.semaphore_signal(barrier, inc=1, device_id=ahead(slot), device_id_type=MESH)
-        return carry
-
-    lax.fori_loop(1, 128, greet, 0)
+    for slot in range(1, 128):
+        pl.semaphore_signal(barrier, inc=1, device_id=targets[slot], device_id_type=LOGICAL)
+
+    dispatch_steps(rank_ref, slot_ref, coord_ref, send, key_ref, meta_ref)
+
     pl.semaphore_wait(barrier, 127)
-
-    pltpu.make_async_copy(send.at[:, me], got.at[:, 0], got_sems.at[0]).start()
-
-    def ship(slot, carry):
-        where = ahead(slot)
+    pltpu.make_async_copy(send.at[:, pl.ds(me, 1)], got.at[:, pl.ds(0, 1)], got_sems.at[0]).start()
+    for slot in range(1, 128):
         pltpu.make_async_remote_copy(
-            src_ref=send.at[:, number(where)],
-            dst_ref=got.at[:, slot],
+            src_ref=send.at[:, pl.ds(targets[slot], 1)],
+            dst_ref=got.at[:, pl.ds(slot, 1)],
             send_sem=send_sem,
             recv_sem=got_sems.at[slot // CHUNK],
-            device_id=where,
-            device_id_type=MESH,
+            device_id=targets[slot],
+            device_id_type=LOGICAL,
         ).start()
-        return carry
-
-    lax.fori_loop(1, 128, ship, 0)
 
     lane = lax.broadcasted_iota(jnp.int32, (1, 128), 1) >> 5
     element = lax.broadcasted_iota(jnp.int32, (128, 256), 0)
@@ -271,9 +303,9 @@
         base = chunk * CHUNK
         block = got.at[:, pl.ds(base, CHUNK)]
         pltpu.make_async_copy(block, block, got_sems.at[chunk]).wait()
-        rows = [[got[a, base + i] for a in range(4)] for i in range(CHUNK)]
+        rows = [[got[a, pl.ds(base + i, 1), :] for a in range(4)] for i in range(CHUNK)]
         for i in range(CHUNK // 4):
-            ends = [got[4, base + 4 * i + w] for w in range(4)]
+            ends = [got[4, pl.ds(base + 4 * i + w, 1), :] for w in range(4)]
             tail = []
             for a in range(4):
                 row = None
@@ -302,7 +334,7 @@
                 pieces = [value[f : f + 1, 128 * h : 128 * h + 128] for f in range(4)]
                 if i + h < CHUNK:
                     for f in range(4):
-                        vals[f, base + i + h] = pieces[f]
+                        vals[f, pl.ds(base + i + h, 1), :] = pieces[f]
                 else:
                     found.append(pieces)
         for i in range(CHUNK // 4):
@@ -312,29 +344,30 @@
                     turn = (32 * (f - w)) % 128
                     x = pltpu.roll(found[i][f], turn, 1) if turn else found[i][f]
                     row = x if row is None else jnp.where(lane == f, x, row)
-                vals[4, base + 4 * i + w] = row
-
-        def answer(slot, inner):
-            where = behind(slot)
-
-            @pl.when(slot == 0)
-            def _():
-                pltpu.make_async_copy(vals.at[:, 0], back.at[:, me], back_sem).start()
-
-            @pl.when(slot > 0)
-            def _():
+                vals[4, pl.ds(base + 4 * i + w, 1), :] = row
+
+        for i in range(CHUNK):
+            dx, dy = steps(base // 16, (i // 8) % 2)
+            where = behind(dx, dy, i % 8)
+
+            def local_answer():
+                pltpu.make_async_copy(vals.at[:, pl.ds(0, 1)], back.at[:, pl.ds(me, 1)], back_sem).start()
+
+            def answer():
                 pltpu.make_async_remote_copy(
-                    src_ref=vals.at[:, slot],
-                    dst_ref=back.at[:, me],
+                    src_ref=vals.at[:, pl.ds(base + i, 1)],
+                    dst_ref=back.at[:, pl.ds(me, 1)],
                     send_sem=value_sem,
                     recv_sem=back_sem,
                     device_id=where,
-                    device_id_type=MESH,
+                    device_id_type=LOGICAL,
                 ).start()
 
-            return inner
-
-        lax.fori_loop(base, base + CHUNK, answer, 0)
+            if i == 0:
+                pl.when(chunk == 0)(local_answer)
+                pl.when(chunk > 0)(answer)
+            else:
+                answer()
         return carry
 
     lax.fori_loop(0, 128 // CHUNK, work, 0)
@@ -345,27 +378,20 @@
     pltpu.make_async_copy(back, back, back_sem).wait()
 
 
-def dispatch(rank, slot, coords):
+def exchange(rank, slot, coords, table):
     return pl.pallas_call(
-        dispatch_kernel,
+        exchange_kernel,
+        in_specs=[pl.BlockSpec(memory_space=pltpu.VMEM)] * 4,
+        out_specs=[pl.BlockSpec(memory_space=pltpu.VMEM)] * 3,
         out_shape=[
             jax.ShapeDtypeStruct((5, 128, 128), jnp.float32),
             jax.ShapeDtypeStruct((NV, 8, 128), jnp.int32),
             jax.ShapeDtypeStruct((2, 8, 128), jnp.int32),
         ],
-        name="dispatch",
-    )(rank, slot, coords)
-
-
-def exchange(send, table):
-    return pl.pallas_call(
-        exchange_kernel,
-        in_specs=[pl.BlockSpec(memory_space=pltpu.VMEM)] * 2,
-        out_specs=pl.BlockSpec(memory_space=pltpu.VMEM),
-        out_shape=jax.ShapeDtypeStruct((5, 128, 1, 128), jnp.float32),
         scratch_shapes=[
-            pltpu.VMEM((5, 128, 1, 128), jnp.float32),
-            pltpu.VMEM((5, 128, 1, 128), jnp.float32),
+            pltpu.VMEM((5, 128, 128), jnp.float32),
+            pltpu.VMEM((5, 128, 128), jnp.float32),
+            pltpu.VMEM((5, 128, 128), jnp.float32),
             pltpu.SemaphoreType.DMA,
             pltpu.SemaphoreType.DMA((128 // CHUNK,)),
             pltpu.SemaphoreType.DMA,
@@ -373,13 +399,13 @@
         ],
         compiler_params=pltpu.CompilerParams(collective_id=0, has_side_effects=True),
         name="exchange",
-    )(send, table)
+    )(rank, slot, coords, table)
 
 
 def give_back(back, key, meta):
     return pl.pallas_call(
         return_kernel,
-        out_shape=jax.ShapeDtypeStruct((4, NV, 8, 128), jnp.float32),
+        out_shape=jax.ShapeDtypeStruct((128, 4, 128), jnp.float32),
         name="give_back",
     )(back, key, meta)
 
@@ -387,11 +413,10 @@
 def local(fields, coordinates, element_rank, element_slot):
     rank = element_rank.reshape(NV, 8, 128)
     slot = element_slot.reshape(NV, 8, 128)
-    coords = coordinates.reshape(3, NV, 8, 128)
+    coords = coordinates.reshape(3, 128, 128).transpose(1, 0, 2)
     table = fields.reshape(128, 256, 8).transpose(1, 2, 0).reshape(256, 1024)
-    send, key, meta = dispatch(rank, slot, coords)
-    back = exchange(send.reshape(5, 128, 1, 128), table).reshape(5, 128, 128)
-    return give_back(back, key, meta).reshape(4, 16384)
+    back, key, meta = exchange(rank, slot, coords, table)
+    return give_back(back, key, meta).transpose(1, 0, 2).reshape(4, 16384)
 
 
 def solution(mesh):

time: 57.8 us -> 45.4 us (0.79)
  Pallas kernels: 52.9 us -> 43 us
  local copies, waits for them, and re-layouts: 4.68 us -> 2.2 us
    pallas_call x2 -> x1, Pallas kernels: 12.4 us -> 5.9 us  [give_back(): pl.pallas_call(return_kernel, out_shape=jax.ShapeDtypeStruct((128, 4, 128...]
    pallas_call x1, Pallas kernels: 40.5 us -> 37.1 us  [exchange(): pl.pallas_call(exchange_kernel, in_specs=[pl.BlockSpec(memory_space=pltpu...]
    unnamed x6 -> x2, local copies, waits for them, and re-layouts: 4.68 us -> 2.2 us
where the time goes in v3:
time: 45.4 us; the launch traced here: 45.2 us
  Pallas kernels  43 us (95%)
  local copies, waits for them, and re-layouts  2.2 us (5%)
    pallas_call x1, Pallas kernels, exchange(): pl.pallas_call(exchange_kernel, in_specs=[pl.BlockSpec(memory_space=pltpu...  37.1 us
    pallas_call x1, Pallas kernels, give_back(): pl.pallas_call(return_kernel, out_shape=jax.ShapeDtypeStruct((128, 4, 128...  5.9 us
    unnamed x2, local copies, waits for them, and re-layouts  2.2 us

profile of v3, /device:TPU:1, one launch (start us, length us, event | category | flops | bytes accessed | tf_op | source)
XLA Modules:
  0.0 45.2 jit_solution(2956222611275266061)
XLA Ops:
  0.0 1.3 %copy.6 = bf16[128,2048]{0,1:T(8,128)(2,1)S(1)} copy(bf16[128,2048]{1,0:T(8,128)(2,1)} %param.4) | data formatting | bytes 1048576 | tf_op args[0]
  1.3 0.9 %copy.9 = bf16[32,8,8,128]{3,1,2,0:T(8,128)(2,1)} copy(bf16[32,8,8,128]{3,2,1,0:T(8,128)(2,1)S(1)} %bitcast.16) | data formatting | bytes 1048576
  2.2 37.1 %exchange.1 = (f32[5,128,128]{2,1,0:T(8,128)}, s32[16,8,128]{2,1,0:T(8,128)}, s32[2,8,128]{2,1,0:T(8,128)}) custom-call(s32[16,8,128]{2,1,0:T(8,128)} %bitcast.18, s32[16,8,128]{2,1,0:T(8,128)} %bitcast.19, f32[128,3,128]{2,1,0:T(4,128)} %bitcast.17, bf16[256,1024]{1,0:T(8,128)(2,1)} %bitcast.15), custom_call_target="tpu_custom_call" | custom-call | tf_op jit(solution)/shard_map/exchange/pallas_call | solution.py:382
  39.3 5.9 %give_back.1 = f32[128,4,128]{2,1,0:T(4,128)} custom-call(f32[5,128,128]{2,1,0:T(8,128)} %get-tuple-element.8.back_ref, s32[16,8,128]{2,1,0:T(8,128)} %get-tuple-element.9.key_ref, s32[2,8,128]{2,1,0:T(8,128)} %get-tuple-element.10.meta_ref), custom_call_target="tpu_custom_call" | custom-call | tf_op jit(solution)/shard_map/give_back/pallas_call | solution.py:406

commit v4 on v3

--- a/solution.py
+++ b/solution.py
@@ -10,7 +10,6 @@
 
 AXES = ("gx", "gy", "gz")
 LOGICAL = pl.DeviceIdType.LOGICAL
-CHUNK = 16
 LEVELS = (1 << 21) - 1
 NV = 16
 
@@ -261,51 +260,155 @@
     return factors[0] * scale
 
 
+def hops(step):
+    ring = (0, 1, 2, 1)
+    dx, dy, dz = step
+    return ring[dx] + ring[dy] + (ring[dz // 2] + ring[(dz + 1) // 2 % 4]) / 2
+
+
+def slot_order():
+    order = sorted(((x, y, z) for x in range(4) for y in range(4) for z in range(8)), key=hops)
+    return order[16:64] + order[96:] + order[64:96] + order[:16]
+
+
+CHUNKS = (16, 32, 32, 32, 16)
+STEPS = slot_order()
+OWN = STEPS.index((0, 0, 0))
+
+
+def fill_table(fields, table):
+    q = lax.broadcasted_iota(jnp.int32, (256, 256), 0)
+    k = lax.broadcasted_iota(jnp.int32, (256, 256), 1)
+    mover = ((q % 32) * 8 + q // 32 == k).astype(jnp.float32).astype(jnp.bfloat16)
+    for g in range(8):
+        block = lax.dot_general(
+            mover,
+            fields[:, g * 256 : g * 256 + 256],
+            (((1,), (1,)), ((), ())),
+            preferred_element_type=jnp.float32,
+        ).astype(jnp.bfloat16)
+        for c in range(8):
+            table[g * 32 : g * 32 + 32, c * 128 : c * 128 + 128] = block[c * 32 : c * 32 + 32]
+
+
 def exchange_kernel(
-    rank_ref, slot_ref, coord_ref, table, back, key_ref, meta_ref, send, got, vals, send_sem, got_sems, value_sem, back_sem
+    rank_hbm,
+    slot_hbm,
+    coord_hbm,
+    fields_hbm,
+    back,
+    key_ref,
+    meta_ref,
+    rank_ref,
+    slot_ref,
+    coord_ref,
+    fields,
+    send,
+    got,
+    vals,
+    table,
+    load_sems,
+    send_sem,
+    got_sems,
+    value_sem,
+    back_sem,
 ):
     gx, gy, gz = (lax.axis_index(name) for name in AXES)
     me = gx * 32 + gy * 8 + gz
-
-    def ahead(dx, dy, dz):
-        return ((gx + dx) % 4) * 32 + ((gy + dy) % 4) * 8 + (gz + dz) % 8
-
-    def behind(dx, dy, dz):
-        return ((gx + 4 - dx) % 4) * 32 + ((gy + 4 - dy) % 4) * 8 + (gz + 8 - dz) % 8
-
-    def steps(chunk, half):
-        dx = chunk // 2
-        return dx, ((chunk + dx) % 2) * 2 + half
-
-    targets = [ahead(*steps(slot // 16, (slot // 8) % 2), slot % 8) for slot in range(128)]
+    xs = [((gx + k) % 4) * 32 for k in range(4)]
+    ys = [((gy + k) % 4) * 8 for k in range(4)]
+    zs = [(gz + k) % 8 for k in range(8)]
+
+    def ahead(slot):
+        dx, dy, dz = STEPS[slot]
+        return xs[dx] + ys[dy] + zs[dz]
+
+    def behind(slot):
+        dx, dy, dz = STEPS[slot]
+        return xs[-dx % 4] + ys[-dy % 4] + zs[-dz % 8]
+
     barrier = pltpu.get_barrier_semaphore()
-    for slot in range(1, 128):
-        pl.semaphore_signal(barrier, inc=1, device_id=targets[slot], device_id_type=LOGICAL)
-
+    others = [slot for slot in range(128) if slot != OWN]
+
+    def greet():
+        for slot in others:
+            pl.semaphore_signal(barrier, inc=1, device_id=ahead(slot), device_id_type=LOGICAL)
+
+    loads = [
+        pltpu.make_async_copy(source, place, load_sems.at[i])
+        for i, (source, place) in enumerate(
+            [(rank_hbm, rank_ref), (slot_hbm, slot_ref), (coord_hbm, coord_ref), (fields_hbm, fields)]
+        )
+    ]
+    for load in loads:
+        load.start()
+    greet()
+    for load in loads:
+        load.wait()
+    fill_table(fields, table)
     dispatch_steps(rank_ref, slot_ref, coord_ref, send, key_ref, meta_ref)
-
     pl.semaphore_wait(barrier, 127)
-    pltpu.make_async_copy(send.at[:, pl.ds(me, 1)], got.at[:, pl.ds(0, 1)], got_sems.at[0]).start()
-    for slot in range(1, 128):
+
+    starts = [sum(CHUNKS[:i]) for i in range(len(CHUNKS))]
+    chunk_of = [i for i, count in enumerate(CHUNKS) for _ in range(count)]
+
+    def ship(slot):
+        if slot == OWN:
+            pltpu.make_async_copy(
+                send.at[:, pl.ds(me, 1)], got.at[:, pl.ds(slot, 1)], got_sems.at[chunk_of[slot]]
+            ).start()
+            return
+        where = ahead(slot)
         pltpu.make_async_remote_copy(
-            src_ref=send.at[:, pl.ds(targets[slot], 1)],
+            src_ref=send.at[:, pl.ds(where, 1)],
             dst_ref=got.at[:, pl.ds(slot, 1)],
             send_sem=send_sem,
-            recv_sem=got_sems.at[slot // CHUNK],
-            device_id=targets[slot],
+            recv_sem=got_sems.at[chunk_of[slot]],
+            device_id=where,
             device_id_type=LOGICAL,
         ).start()
 
+    def answer(slot):
+        if slot == OWN:
+            pltpu.make_async_copy(vals.at[:, pl.ds(slot, 1)], back.at[:, pl.ds(me, 1)], back_sem).start()
+            return
+        pltpu.make_async_remote_copy(
+            src_ref=vals.at[:, pl.ds(slot, 1)],
+            dst_ref=back.at[:, pl.ds(me, 1)],
+            send_sem=value_sem,
+            recv_sem=back_sem,
+            device_id=behind(slot),
+            device_id_type=LOGICAL,
+        ).start()
+
+    for slot in range(128):
+        ship(slot)
+
     lane = lax.broadcasted_iota(jnp.int32, (1, 128), 1) >> 5
     element = lax.broadcasted_iota(jnp.int32, (128, 256), 0)
 
-    def work(chunk, carry):
-        base = chunk * CHUNK
-        block = got.at[:, pl.ds(base, CHUNK)]
+    def pair(rows):
+        r, s, t, slot = [jnp.concatenate([rows[0][a], rows[1][a]], axis=1) for a in range(4)]
+        weight_r, weight_s, weight_t = node_weights(r), node_weights(s), node_weights(t)
+        onehot = (element == slot.astype(jnp.int32)).astype(jnp.float32).astype(jnp.bfloat16)
+        onehot = onehot.reshape(8, 16, 256)
+        parts = []
+        for c in range(8):
+            w = jnp.broadcast_to(weight_t[c : c + 1], (16, 256)).astype(jnp.bfloat16)
+            parts.append((onehot * w[None]).reshape(128, 256))
+        along = jnp.dot(table[...], jnp.concatenate(parts, axis=0), preferred_element_type=jnp.float32)
+        along = along.reshape(4, 8, 8, 256)
+        along = jnp.sum(along * weight_r[None, :, None, :], axis=1)
+        value = jnp.sum(along * weight_s[None], axis=1)
+        return [[value[f : f + 1, 128 * h : 128 * h + 128] for f in range(4)] for h in range(2)]
+
+    for chunk, count in enumerate(CHUNKS):
+        base = starts[chunk]
+        block = got.at[:, pl.ds(base, count)]
         pltpu.make_async_copy(block, block, got_sems.at[chunk]).wait()
-        rows = [[got[a, pl.ds(base + i, 1), :] for a in range(4)] for i in range(CHUNK)]
-        for i in range(CHUNK // 4):
-            ends = [got[4, pl.ds(base + 4 * i + w, 1), :] for w in range(4)]
+        tails = []
+        for i in range(count // 4):
+            ends = [got[4, base + 4 * i + w : base + 4 * i + w + 1, :] for w in range(4)]
             tail = []
             for a in range(4):
                 row = None
@@ -314,63 +417,25 @@
                     x = pltpu.roll(ends[w], turn, 1) if turn else ends[w]
                     row = x if row is None else jnp.where(lane == w, x, row)
                 tail.append(row)
-            rows.append(tail)
+            tails.append(tail)
         found = []
-        for i in range(0, len(rows), 2):
-            r, s, t, slot = [jnp.concatenate([rows[i][a], rows[i + 1][a]], axis=1) for a in range(4)]
-            weight_r, weight_s, weight_t = node_weights(r), node_weights(s), node_weights(t)
-            onehot = (element == slot.astype(jnp.int32)).astype(jnp.float32).astype(jnp.bfloat16)
-            onehot = onehot.reshape(8, 16, 256)
-            parts = []
-            for c in range(8):
-                w = jnp.broadcast_to(weight_t[c : c + 1], (16, 256)).astype(jnp.bfloat16)
-                parts.append((onehot * w[None]).reshape(128, 256))
-            picker = jnp.concatenate(parts, axis=0)
-            along = jnp.dot(table[...], picker, preferred_element_type=jnp.float32)
-            along = along.reshape(4, 8, 8, 256)
-            along = jnp.sum(along * weight_r[None, :, None, :], axis=1)
-            value = jnp.sum(along * weight_s[None], axis=1)
-            for h in range(2):
-                pieces = [value[f : f + 1, 128 * h : 128 * h + 128] for f in range(4)]
-                if i + h < CHUNK:
-                    for f in range(4):
-                        vals[f, pl.ds(base + i + h, 1), :] = pieces[f]
-                else:
-                    found.append(pieces)
-        for i in range(CHUNK // 4):
+        for i in range(0, count // 4, 2):
+            found += pair(tails[i : i + 2])
+        for i in range(count // 4):
             for w in range(4):
                 row = None
                 for f in range(4):
                     turn = (32 * (f - w)) % 128
                     x = pltpu.roll(found[i][f], turn, 1) if turn else found[i][f]
                     row = x if row is None else jnp.where(lane == f, x, row)
-                vals[4, pl.ds(base + 4 * i + w, 1), :] = row
-
-        for i in range(CHUNK):
-            dx, dy = steps(base // 16, (i // 8) % 2)
-            where = behind(dx, dy, i % 8)
-
-            def local_answer():
-                pltpu.make_async_copy(vals.at[:, pl.ds(0, 1)], back.at[:, pl.ds(me, 1)], back_sem).start()
-
-            def answer():
-                pltpu.make_async_remote_copy(
-                    src_ref=vals.at[:, pl.ds(base + i, 1)],
-                    dst_ref=back.at[:, pl.ds(me, 1)],
-                    send_sem=value_sem,
-                    recv_sem=back_sem,
-                    device_id=where,
-                    device_id_type=LOGICAL,
-                ).start()
-
-            if i == 0:
-                pl.when(chunk == 0)(local_answer)
-                pl.when(chunk > 0)(answer)
-            else:
-                answer()
-        return carry
-
-    lax.fori_loop(0, 128 // CHUNK, work, 0)
+                vals[4, base + 4 * i + w : base + 4 * i + w + 1, :] = row
+        for i in range(base, base + count, 2):
+            found = pair([[got[a, i + h : i + h + 1, :] for a in range(4)] for h in range(2)])
+            for h in range(2):
+                for f in range(4):
+                    vals[f, i + h : i + h + 1, :] = found[h][f]
+        for i in range(base, base + count):
+            answer(i)
     sent = send.at[:, pl.ds(0, 127)]
     pltpu.make_async_copy(sent, sent, send_sem).wait()
     told = vals.at[:, pl.ds(0, 127)]
@@ -378,10 +443,10 @@
     pltpu.make_async_copy(back, back, back_sem).wait()
 
 
-def exchange(rank, slot, coords, table):
+def exchange(rank, slot, coords, fields):
     return pl.pallas_call(
         exchange_kernel,
-        in_specs=[pl.BlockSpec(memory_space=pltpu.VMEM)] * 4,
+        in_specs=[pl.BlockSpec(memory_space=pltpu.HBM)] * 4,
         out_specs=[pl.BlockSpec(memory_space=pltpu.VMEM)] * 3,
         out_shape=[
             jax.ShapeDtypeStruct((5, 128, 128), jnp.float32),
@@ -389,17 +454,23 @@
             jax.ShapeDtypeStruct((2, 8, 128), jnp.int32),
         ],
         scratch_shapes=[
+            pltpu.VMEM((NV, 8, 128), jnp.int32),
+            pltpu.VMEM((NV, 8, 128), jnp.int32),
+            pltpu.VMEM((128, 3, 128), jnp.float32),
+            pltpu.VMEM((128, 2048), jnp.bfloat16),
             pltpu.VMEM((5, 128, 128), jnp.float32),
             pltpu.VMEM((5, 128, 128), jnp.float32),
             pltpu.VMEM((5, 128, 128), jnp.float32),
+            pltpu.VMEM((256, 1024), jnp.bfloat16),
+            pltpu.SemaphoreType.DMA((4,)),
             pltpu.SemaphoreType.DMA,
-            pltpu.SemaphoreType.DMA((128 // CHUNK,)),
+            pltpu.SemaphoreType.DMA((len(CHUNKS),)),
             pltpu.SemaphoreType.DMA,
             pltpu.SemaphoreType.DMA,
         ],
         compiler_params=pltpu.CompilerParams(collective_id=0, has_side_effects=True),
         name="exchange",
-    )(rank, slot, coords, table)
+    )(rank, slot, coords, fields)
 
 
 def give_back(back, key, meta):
@@ -414,8 +485,7 @@
     rank = element_rank.reshape(NV, 8, 128)
     slot = element_slot.reshape(NV, 8, 128)
     coords = coordinates.reshape(3, 128, 128).transpose(1, 0, 2)
-    table = fields.reshape(128, 256, 8).transpose(1, 2, 0).reshape(256, 1024)
-    back, key, meta = exchange(rank, slot, coords, table)
+    back, key, meta = exchange(rank, slot, coords, fields)
     return give_back(back, key, meta).transpose(1, 0, 2).reshape(4, 16384)
 
 

time: 45.4 us -> 40 us (0.88)
  Pallas kernels: 43 us -> 39.9 us
  local copies, waits for them, and re-layouts: 2.2 us -> 0 us
    pallas_call x1, Pallas kernels: 37.1 us -> 34 us  [exchange(): pl.pallas_call(exchange_kernel, in_specs=[pl.BlockSpec(memory_space=pltpu...]
    unnamed x2 -> x0, local copies, waits for them, and re-layouts: 2.2 us -> none
where the time goes in v4:
time: 40 us; the launch traced here: 39.9 us
  Pallas kernels  39.9 us (100%)
    pallas_call x1, Pallas kernels, exchange(): pl.pallas_call(exchange_kernel, in_specs=[pl.BlockSpec(memory_space=pltpu...  34 us
    pallas_call x1, Pallas kernels, give_back(): pl.pallas_call(return_kernel, out_shape=jax.ShapeDtypeStruct((128, 4, 128...  5.9 us

profile of v4, /device:TPU:1, one launch (start us, length us, event | category | flops | bytes accessed | tf_op | source)
XLA Modules:
  0.0 39.9 jit_solution(13731375701677461449)
XLA Ops:
  0.0 34.0 %exchange.1 = (f32[5,128,128]{2,1,0:T(8,128)}, s32[16,8,128]{2,1,0:T(8,128)}, s32[2,8,128]{2,1,0:T(8,128)}) custom-call(s32[16,8,128]{2,1,0:T(8,128)} %bitcast.9, s32[16,8,128]{2,1,0:T(8,128)} %bitcast.10, f32[128,3,128]{2,1,0:T(4,128)} %bitcast.8, bf16[128,2048]{1,0:T(8,128)(2,1)} %fields_hbm.1), custom_call_target="tpu_custom_call" | custom-call | tf_op jit(solution)/shard_map/exchange/pallas_call | solution.py:447
  34.0 5.9 %give_back.1 = f32[128,4,128]{2,1,0:T(4,128)} custom-call(f32[5,128,128]{2,1,0:T(8,128)} %get-tuple-element.8.back_ref, s32[16,8,128]{2,1,0:T(8,128)} %get-tuple-element.9.key_ref, s32[2,8,128]{2,1,0:T(8,128)} %get-tuple-element.10.meta_ref), custom_call_target="tpu_custom_call" | custom-call | tf_op jit(solution)/shard_map/give_back/pallas_call | solution.py:477

commit v5 on v4

--- a/solution.py
+++ b/solution.py
@@ -1,5 +1,3 @@
-import functools
-
 import jax
 import jax.numpy as jnp
 import numpy as np
@@ -81,6 +79,90 @@
                     x, y = arrs[a][v], arrs[a][w]
                     arrs[a][v] = jnp.where(swap, y, x)
                     arrs[a][w] = jnp.where(swap, x, y)
+    return arrs
+
+
+def row_bit(b, s_io):
+    return ((s_io >> (b - 4)) & 1) == 1
+
+
+def plan_route(labels, lane_plan, swap_plan):
+    s_io, l_io = iotas()
+    items = list(labels)
+    note = 0
+
+    def lane_bit(b):
+        return ((l_io >> (b - 7)) & 1) == 1
+
+    for k in range(1, 15):
+        down = None
+        if 4 <= k < 14:
+            down = row_bit(k, s_io) if k < 7 else lane_bit(k)
+        origin = [l_io] * NV
+        for j in range(k - 1, 6, -1):
+            upper = lane_bit(j)
+            flip = upper if down is None else jnp.logical_xor(upper, down)
+            for v in range(NV):
+                other = partner(items[v], 1, 1 << (j - 7), upper)
+                there = partner(origin[v], 1, 1 << (j - 7), upper)
+                take = jnp.logical_xor(items[v] > other, flip)
+                items[v] = jnp.where(take, other, items[v])
+                origin[v] = jnp.where(take, there, origin[v])
+            yield
+        if k > 7:
+            for v in range(NV):
+                lane_plan[k - 8, v] = origin[v]
+        for j in range(min(k - 1, 6), 3, -1):
+            upper = row_bit(j, s_io)
+            flip = upper if down is None else jnp.logical_xor(upper, down)
+            for v in range(NV):
+                other = partner(items[v], 0, 1 << (j - 4), upper)
+                take = jnp.logical_xor(items[v] > other, flip)
+                items[v] = jnp.where(take, other, items[v])
+                swap_plan[note] = jnp.where(take, 1, 0)
+                note += 1
+            yield
+        for j in range(min(k, 4) - 1, -1, -1):
+            d = 1 << j
+            for v in range(NV):
+                if v & d:
+                    continue
+                x, y = items[v], items[v | d]
+                swap = x < y if k < 4 and (v >> k) & 1 else x > y
+                if down is not None:
+                    swap = jnp.logical_xor(swap, down)
+                items[v], items[v | d] = jnp.where(swap, y, x), jnp.where(swap, x, y)
+                swap_plan[note] = jnp.where(swap, 1, 0)
+                note += 1
+            yield
+
+
+def follow_route(arrs, lane_plan, swap_plan):
+    s_io, _ = iotas()
+    arrs = [list(x) for x in arrs]
+    note = 0
+    for k in range(1, 15):
+        if k > 7:
+            for v in range(NV):
+                idx = lane_plan[k - 8, v]
+                for x in arrs:
+                    x[v] = take_lanes(x[v], idx)
+        for j in range(min(k - 1, 6), 3, -1):
+            upper = row_bit(j, s_io)
+            for v in range(NV):
+                take = swap_plan[note] == 1
+                note += 1
+                for x in arrs:
+                    x[v] = jnp.where(take, partner(x[v], 0, 1 << (j - 4), upper), x[v])
+        for j in range(min(k, 4) - 1, -1, -1):
+            d = 1 << j
+            for v in range(NV):
+                if v & d:
+                    continue
+                swap = swap_plan[note] == 1
+                note += 1
+                for x in arrs:
+                    x[v], x[v | d] = jnp.where(swap, x[v | d], x[v]), jnp.where(swap, x[v], x[v | d])
     return arrs
 
 
@@ -181,7 +263,7 @@
     send_ref[4] = jnp.concatenate([x for a in range(4) for x in split[a][NV:]], axis=0).T
 
 
-def return_kernel(back_ref, key_ref, meta_ref, out_ref):
+def return_steps(back_ref, key_ref, meta_ref, out_ref, lane_plan, swap_plan):
     s_io, l_io = iotas()
     column, shift = meta_ref[0], meta_ref[1]
     keys = [key_ref[v] for v in range(NV)]
@@ -225,28 +307,10 @@
             x = [take_lanes(table[k][v], ranks[v]) for k in range(3)]
             picked.append(jnp.where(blocks[v] == 0, x[0], jnp.where(blocks[v] == 1, x[1], x[2])))
         values.append(picked)
-    largest = functools.reduce(jnp.maximum, [jnp.abs(x) for picked in values for x in picked])
-    largest = jnp.maximum(jnp.max(jnp.max(largest, axis=0, keepdims=True), axis=1, keepdims=True), 1e-30)
-    grow = jnp.broadcast_to(524287.0 / largest, (8, 128))
-    shrink = jnp.broadcast_to(largest / 524287.0, (8, 128))
-    words = [[], [], []]
-    for v in range(NV):
-        q = [(values[f][v] * grow + 524288.5).astype(jnp.int32) for f in range(4)]
-        low = ((q[0] & 15) << 12) | ((q[1] & 15) << 8) | ((q[2] & 15) << 4) | (q[3] & 15)
-        words[0].append(((keys[v] & 16383) << 16) | low)
-        words[1].append(((q[0] >> 4) << 16) | (q[1] >> 4))
-        words[2].append(((q[2] >> 4) << 16) | (q[3] >> 4))
-    words = network(words)
-    for v in range(NV):
-        low, first, second = [words[a][v] for a in range(3)]
-        q = [
-            (right(first, 16) << 4) | ((low >> 12) & 15),
-            ((first & 65535) << 4) | ((low >> 8) & 15),
-            (right(second, 16) << 4) | ((low >> 4) & 15),
-            ((second & 65535) << 4) | (low & 15),
-        ]
-        for f in range(4):
-            out_ref[8 * v : 8 * v + 8, f, :] = (q[f] - 524288).astype(jnp.float32) * shrink
+    values = follow_route(values, lane_plan, swap_plan)
+    for f in range(4):
+        for v in range(NV):
+            out_ref[8 * v : 8 * v + 8, f, :] = values[f][v]
 
 
 def node_weights(coord):
@@ -272,6 +336,7 @@
 
 
 CHUNKS = (16, 32, 32, 32, 16)
+PLAN_STEPS = 2
 STEPS = slot_order()
 OWN = STEPS.index((0, 0, 0))
 
@@ -296,6 +361,7 @@
     slot_hbm,
     coord_hbm,
     fields_hbm,
+    out_ref,
     back,
     key_ref,
     meta_ref,
@@ -307,6 +373,8 @@
     got,
     vals,
     table,
+    lane_plan,
+    swap_plan,
     load_sems,
     send_sem,
     got_sems,
@@ -387,7 +455,11 @@
     lane = lax.broadcasted_iota(jnp.int32, (1, 128), 1) >> 5
     element = lax.broadcasted_iota(jnp.int32, (128, 256), 0)
 
+    planning = plan_route([key_ref[v] & 16383 for v in range(NV)], lane_plan, swap_plan)
+
     def pair(rows):
+        for _ in range(PLAN_STEPS):
+            next(planning, None)
         r, s, t, slot = [jnp.concatenate([rows[0][a], rows[1][a]], axis=1) for a in range(4)]
         weight_r, weight_s, weight_t = node_weights(r), node_weights(s), node_weights(t)
         onehot = (element == slot.astype(jnp.int32)).astype(jnp.float32).astype(jnp.bfloat16)
@@ -441,19 +513,19 @@
     told = vals.at[:, pl.ds(0, 127)]
     pltpu.make_async_copy(told, told, value_sem).wait()
     pltpu.make_async_copy(back, back, back_sem).wait()
+    return_steps(back, key_ref, meta_ref, out_ref, lane_plan, swap_plan)
 
 
 def exchange(rank, slot, coords, fields):
     return pl.pallas_call(
         exchange_kernel,
         in_specs=[pl.BlockSpec(memory_space=pltpu.HBM)] * 4,
-        out_specs=[pl.BlockSpec(memory_space=pltpu.VMEM)] * 3,
-        out_shape=[
-            jax.ShapeDtypeStruct((5, 128, 128), jnp.float32),
-            jax.ShapeDtypeStruct((NV, 8, 128), jnp.int32),
-            jax.ShapeDtypeStruct((2, 8, 128), jnp.int32),
-        ],
+        out_specs=pl.BlockSpec(memory_space=pltpu.VMEM),
+        out_shape=jax.ShapeDtypeStruct((128, 4, 128), jnp.float32),
         scratch_shapes=[
+            pltpu.VMEM((5, 128, 128), jnp.float32),
+            pltpu.VMEM((NV, 8, 128), jnp.int32),
+            pltpu.VMEM((2, 8, 128), jnp.int32),
             pltpu.VMEM((NV, 8, 128), jnp.int32),
             pltpu.VMEM((NV, 8, 128), jnp.int32),
             pltpu.VMEM((128, 3, 128), jnp.float32),
@@ -462,6 +534,8 @@
             pltpu.VMEM((5, 128, 128), jnp.float32),
             pltpu.VMEM((5, 128, 128), jnp.float32),
             pltpu.VMEM((256, 1024), jnp.bfloat16),
+            pltpu.VMEM((7, NV, 8, 128), jnp.int32),
+            pltpu.VMEM((832, 8, 128), jnp.int32),
             pltpu.SemaphoreType.DMA((4,)),
             pltpu.SemaphoreType.DMA,
             pltpu.SemaphoreType.DMA((len(CHUNKS),)),
@@ -473,20 +547,11 @@
     )(rank, slot, coords, fields)
 
 
-def give_back(back, key, meta):
-    return pl.pallas_call(
-        return_kernel,
-        out_shape=jax.ShapeDtypeStruct((128, 4, 128), jnp.float32),
-        name="give_back",
-    )(back, key, meta)
-
-
 def local(fields, coordinates, element_rank, element_slot):
     rank = element_rank.reshape(NV, 8, 128)
     slot = element_slot.reshape(NV, 8, 128)
     coords = coordinates.reshape(3, 128, 128).transpose(1, 0, 2)
-    back, key, meta = exchange(rank, slot, coords, fields)
-    return give_back(back, key, meta).transpose(1, 0, 2).reshape(4, 16384)
+    return exchange(rank, slot, coords, fields).transpose(1, 0, 2).reshape(4, 16384)
 
 
 def solution(mesh):

time: 40 us -> 39.1 us (0.978)
  Pallas kernels: 39.9 us -> 37.3 us
  local copies, waits for them, and re-layouts: 0 us -> 1.67 us
    pallas_call x1 -> x0, Pallas kernels: 5.9 us -> none  [give_back(): pl.pallas_call(return_kernel, out_shape=jax.ShapeDtypeStruct((128, 4, 128...]
    pallas_call x1, Pallas kernels: 34 us -> 37.3 us  [exchange(): pl.pallas_call(exchange_kernel, in_specs=[pl.BlockSpec(memory_space=pltpu...]
    unnamed x0 -> x1, local copies, waits for them, and re-layouts: none -> 1.67 us
where the time goes in v5:
time: 39.1 us; the launch traced here: 39 us
  Pallas kernels  37.3 us (95%)
  local copies, waits for them, and re-layouts  1.67 us (4%)
    pallas_call x1, Pallas kernels, exchange(): pl.pallas_call(exchange_kernel, in_specs=[pl.BlockSpec(memory_space=pltpu...  37.3 us
    unnamed x1, local copies, waits for them, and re-layouts  1.67 us

profile of v5, /device:TPU:1, one launch (start us, length us, event | category | flops | bytes accessed | tf_op | source)
XLA Modules:
  0.0 39.0 jit_solution(3094280303261529563)
XLA Ops:
  0.0 37.3 %exchange.1 = f32[128,4,128]{2,1,0:T(4,128)} custom-call(s32[16,8,128]{2,1,0:T(8,128)} %bitcast.10, s32[16,8,128]{2,1,0:T(8,128)} %bitcast.11, f32[128,3,128]{2,1,0:T(4,128)} %bitcast.9, bf16[128,2048]{1,0:T(8,128)(2,1)} %fields_hbm.1), custom_call_target="tpu_custom_call" | custom-call | tf_op jit(solution)/shard_map/exchange/pallas_call | solution.py:520
  37.3 1.7 %copy.6 = f32[4,16384]{1,0:T(4,128)} copy(f32[4,16384]{1,0:T(4,128)} %bitcast.8) | data formatting | bytes 524288

commit v6 on v5

--- a/solution.py
+++ b/solution.py
@@ -397,6 +397,7 @@
 
     barrier = pltpu.get_barrier_semaphore()
     others = [slot for slot in range(128) if slot != OWN]
+    others.sort(key=lambda slot: -hops(STEPS[slot]))
 
     def greet():
         for slot in others:
@@ -506,14 +507,14 @@
             for h in range(2):
                 for f in range(4):
                     vals[f, i + h : i + h + 1, :] = found[h][f]
-        for i in range(base, base + count):
+        for i in sorted(range(base, base + count), key=lambda slot: -hops(STEPS[slot])):
             answer(i)
+    pltpu.make_async_copy(back, back, back_sem).wait()
+    return_steps(back, key_ref, meta_ref, out_ref, lane_plan, swap_plan)
     sent = send.at[:, pl.ds(0, 127)]
     pltpu.make_async_copy(sent, sent, send_sem).wait()
     told = vals.at[:, pl.ds(0, 127)]
     pltpu.make_async_copy(told, told, value_sem).wait()
-    pltpu.make_async_copy(back, back, back_sem).wait()
-    return_steps(back, key_ref, meta_ref, out_ref, lane_plan, swap_plan)
 
 
 def exchange(rank, slot, coords, fields):

time: 39.1 us -> 39 us (level)
  no operation moved by 1% of the time
where the time goes in v6:
time: 39 us; the launch traced here: 38.9 us
  Pallas kernels  37.2 us (95%)
  local copies, waits for them, and re-layouts  1.67 us (4%)
    pallas_call x1, Pallas kernels, exchange(): pl.pallas_call(exchange_kernel, in_specs=[pl.BlockSpec(memory_space=pltpu...  37.2 us
    unnamed x1, local copies, waits for them, and re-layouts  1.67 us

profile of v6, /device:TPU:1, one launch (start us, length us, event | category | flops | bytes accessed | tf_op | source)
XLA Modules:
  0.0 38.9 jit_solution(4374228756874787865)
XLA Ops:
  0.0 37.2 %exchange.1 = f32[128,4,128]{2,1,0:T(4,128)} custom-call(s32[16,8,128]{2,1,0:T(8,128)} %bitcast.10, s32[16,8,128]{2,1,0:T(8,128)} %bitcast.11, f32[128,3,128]{2,1,0:T(4,128)} %bitcast.9, bf16[128,2048]{1,0:T(8,128)(2,1)} %fields_hbm.1), custom_call_target="tpu_custom_call" | custom-call | tf_op jit(solution)/shard_map/exchange/pallas_call | solution.py:521
  37.2 1.7 %copy.6 = f32[4,16384]{1,0:T(4,128)} copy(f32[4,16384]{1,0:T(4,128)} %bitcast.8) | data formatting | bytes 524288

commit v7 on v6

--- a/solution.py
+++ b/solution.py
@@ -42,7 +42,7 @@
     return jnp.where(bit, pltpu.roll(x, d, axis), pltpu.roll(x, n - d, axis))
 
 
-def network(arrs):
+def network(arrs, beside):
     s_io, l_io = iotas()
     arrs = [list(a) for a in arrs]
     count = len(arrs)
@@ -53,6 +53,7 @@
         return ((l_io >> (b - 7)) & 1) == 1
 
     for k in range(1, 15):
+        beside(k)
         down = bit_of(k) if 4 <= k < 14 else None
         for j in range(k - 1, 3, -1):
             axis, d = (0, 1 << (j - 4)) if j < 7 else (1, 1 << (j - 7))
@@ -190,7 +191,7 @@
     return lax.shift_right_logical(x, jnp.full(x.shape, count, jnp.int32))
 
 
-def dispatch_steps(rank_ref, slot_ref, coord_ref, send_ref, key_ref, meta_ref):
+def dispatch_steps(rank_ref, slot_ref, coord_ref, send_ref, key_ref, meta_ref, beside):
     s_io, l_io = iotas()
     words = [[], [], []]
     for v in range(NV):
@@ -199,7 +200,7 @@
         words[0].append(rank_ref[v] * (1 << 21) + slot_ref[v] * (1 << 14) + label)
         words[1].append((r << 11) | (t >> 10))
         words[2].append((s << 11) | (t & 1023))
-    words = network(words)
+    words = network(words, beside)
     keys = words[0]
     for v in range(NV):
         key_ref[v] = keys[v]
@@ -341,19 +342,18 @@
 OWN = STEPS.index((0, 0, 0))
 
 
-def fill_table(fields, table):
+def fill_table(fields, table, g):
     q = lax.broadcasted_iota(jnp.int32, (256, 256), 0)
     k = lax.broadcasted_iota(jnp.int32, (256, 256), 1)
     mover = ((q % 32) * 8 + q // 32 == k).astype(jnp.float32).astype(jnp.bfloat16)
-    for g in range(8):
-        block = lax.dot_general(
-            mover,
-            fields[:, g * 256 : g * 256 + 256],
-            (((1,), (1,)), ((), ())),
-            preferred_element_type=jnp.float32,
-        ).astype(jnp.bfloat16)
-        for c in range(8):
-            table[g * 32 : g * 32 + 32, c * 128 : c * 128 + 128] = block[c * 32 : c * 32 + 32]
+    block = lax.dot_general(
+        mover,
+        fields[:, g * 256 : g * 256 + 256],
+        (((1,), (1,)), ((), ())),
+        preferred_element_type=jnp.float32,
+    ).astype(jnp.bfloat16)
+    for c in range(8):
+        table[g * 32 : g * 32 + 32, c * 128 : c * 128 + 128] = block[c * 32 : c * 32 + 32]
 
 
 def exchange_kernel(
@@ -412,10 +412,19 @@
     for load in loads:
         load.start()
     greet()
-    for load in loads:
+    for load in loads[:3]:
         load.wait()
-    fill_table(fields, table)
-    dispatch_steps(rank_ref, slot_ref, coord_ref, send, key_ref, meta_ref)
+
+    def beside(level):
+        if level == 9:
+            loads[3].wait()
+        if level > 8:
+            fill_table(fields, table, level - 9)
+        if level == 14:
+            fill_table(fields, table, 6)
+            fill_table(fields, table, 7)
+
+    dispatch_steps(rank_ref, slot_ref, coord_ref, send, key_ref, meta_ref, beside)
     pl.semaphore_wait(barrier, 127)
 
     starts = [sum(CHUNKS[:i]) for i in range(len(CHUNKS))]

time: 39 us -> 38.8 us (level)
  no operation moved by 1% of the time
where the time goes in v7:
time: 38.8 us; the launch traced here: 38.7 us
  Pallas kernels  37 us (95%)
  local copies, waits for them, and re-layouts  1.67 us (4%)
    pallas_call x1, Pallas kernels, exchange(): pl.pallas_call(exchange_kernel, in_specs=[pl.BlockSpec(memory_space=pltpu...  37 us
    unnamed x1, local copies, waits for them, and re-layouts  1.67 us

profile of v7, /device:TPU:1, one launch (start us, length us, event | category | flops | bytes accessed | tf_op | source)
XLA Modules:
  0.0 38.7 jit_solution(9444083933829380188)
XLA Ops:
  0.0 37.0 %exchange.1 = f32[128,4,128]{2,1,0:T(4,128)} custom-call(s32[16,8,128]{2,1,0:T(8,128)} %bitcast.10, s32[16,8,128]{2,1,0:T(8,128)} %bitcast.11, f32[128,3,128]{2,1,0:T(4,128)} %bitcast.9, bf16[128,2048]{1,0:T(8,128)(2,1)} %fields_hbm.1), custom_call_target="tpu_custom_call" | custom-call | tf_op jit(solution)/shard_map/exchange/pallas_call | solution.py:530
  37.0 1.7 %copy.6 = f32[4,16384]{1,0:T(4,128)} copy(f32[4,16384]{1,0:T(4,128)} %bitcast.8) | data formatting | bytes 524288
